TPU v7x, 8 devices: a whole 2x2x1 slice. The times are simulated.
8 devices in a mesh: dp: 1 (over z), cp: 8 (over y, x, core).
Axes of the slice: x: 2, y: 2, z: 1, core: 2. Of those that a mesh axis runs over, the one named last changes fastest.
Arguments:
- hidden: bfloat16 [16, 2048, 5120], P('dp', 'cp')
- positions: int32 [16, 2048], P('dp', 'cp')
- w_q: bfloat16 [5120, 32, 128], replicated
- w_k: bfloat16 [5120, 8, 128], replicated
- w_v: bfloat16 [5120, 8, 128], replicated
- w_o: bfloat16 [32, 128, 5120], replicated
Outputs:
- output: bfloat16 [16, 2048, 5120], P('dp', 'cp')
All inputs are finite; a program needn't handle non-finite values.
Results may differ from a plain program's by a relative error of at most 0.00865.
Values are sent between devices in bfloat16 or wider.
A program may use at most 1 GiB of HBM per device.

v0:
```python
import jax
import jax.numpy as jnp
from jax import lax
from jax.sharding import PartitionSpec as P

ROPE_BASE = 500000.0


def rope_tables(positions, head_dim):
    inv_freq = ROPE_BASE ** (-jnp.arange(0, head_dim, 2, dtype=jnp.float32) / head_dim)
    angles = positions.astype(jnp.float32)[..., None] * inv_freq
    angles = jnp.concatenate([angles, angles], axis=-1)
    return jnp.cos(angles)[:, :, None, :], jnp.sin(angles)[:, :, None, :]


def rope_apply(in_vals, cos_tab, sin_tab):
    half_dim = in_vals.shape[-1] // 2
    val_f32 = in_vals.astype(jnp.float32)
    rotated = jnp.concatenate([-val_f32[..., half_dim:], val_f32[..., :half_dim]], axis=-1)
    return (val_f32 * cos_tab + rotated * sin_tab).astype(jnp.bfloat16)


def project_qkv(hidden, positions, w_q, w_k, w_v):
    n_batch, tok_len = hidden.shape[0], hidden.shape[1]
    n_kv, head_dim = w_k.shape[1], w_k.shape[2]
    q_per_kv = w_q.shape[1] // n_kv
    queries = jnp.einsum('bsd,dhe->bshe', hidden, w_q, preferred_element_type=jnp.float32).astype(jnp.bfloat16)
    k_proj = jnp.einsum('bsd,dhe->bshe', hidden, w_k, preferred_element_type=jnp.float32).astype(jnp.bfloat16)
    values = jnp.einsum('bsd,dhe->bshe', hidden, w_v, preferred_element_type=jnp.float32).astype(jnp.bfloat16)
    cos_tab, sin_tab = rope_tables(positions, head_dim)
    queries = rope_apply(queries, cos_tab, sin_tab).reshape(n_batch, tok_len, n_kv, q_per_kv, head_dim)
    k_rot = rope_apply(k_proj, cos_tab, sin_tab)
    return queries, k_rot, values


def empty_state(queries):
    n_batch, tok_len, n_kv, q_per_kv, head_dim = queries.shape
    run_max = jnp.full((n_batch, n_kv, q_per_kv, tok_len), -jnp.inf, jnp.float32)
    run_sum = jnp.zeros((n_batch, n_kv, q_per_kv, tok_len), jnp.float32)
    out_acc = jnp.zeros((n_batch, n_kv, q_per_kv, tok_len, head_dim), jnp.float32)
    return run_max, run_sum, out_acc


def block_update(sm_state, queries, k_blk, v_blk, allowed):
    run_max, run_sum, out_acc = sm_state
    sm_scale = queries.shape[-1] ** -0.5
    scores = jnp.einsum('bqkge,bske->bkgqs', queries, k_blk, preferred_element_type=jnp.float32) * sm_scale
    scores = jnp.where(allowed, scores, -jnp.inf)
    new_max = jnp.maximum(run_max, jnp.max(scores, axis=-1))
    correction = jnp.exp(run_max - new_max)
    p_weights = jnp.exp(scores - new_max[..., None])
    run_sum = run_sum * correction + jnp.sum(p_weights, axis=-1)
    pv_part = jnp.einsum('bkgqs,bske->bkgqe', p_weights.astype(jnp.bfloat16), v_blk, preferred_element_type=jnp.float32)
    out_acc = out_acc * correction[..., None] + pv_part
    return new_max, run_sum, out_acc


def finish(sm_state, hidden, w_o):
    run_sum, out_acc = sm_state[1], sm_state[2]
    n_kv, q_per_kv, head_dim = out_acc.shape[1], out_acc.shape[2], out_acc.shape[4]
    attn_out = (out_acc / run_sum[..., None]).astype(jnp.bfloat16)
    w_o_grp = w_o.reshape(n_kv, q_per_kv, head_dim, w_o.shape[2])
    proj_out = jnp.einsum('clhrf,lhfe->cre', attn_out, w_o_grp, preferred_element_type=jnp.float32)
    return (hidden.astype(jnp.float32) + proj_out).astype(jnp.bfloat16)


def solution(mesh):
    cp_size = mesh.shape['cp']
    shift_pairs = [(j, (j + 1) % cp_size) for j in range(cp_size)]

    def per_device(hidden, positions, w_q, w_k, w_v, w_o):
        queries, k_rot, values = project_qkv(hidden, positions, w_q, w_k, w_v)
        tok_dev = hidden.shape[1]
        my_idx = lax.axis_index('cp')
        row_ids = jnp.arange(tok_dev)[:, None]
        col_ids = jnp.arange(tok_dev)[None, :]
        sm_state = block_update(empty_state(queries), queries, k_rot, values, col_ids <= row_ids)

        def kv_step(step_idx, loop_vals):
            cur_state, k_cur, v_cur = loop_vals
            k_cur = lax.ppermute(k_cur, 'cp', shift_pairs)
            v_cur = lax.ppermute(v_cur, 'cp', shift_pairs)
            src_idx = (my_idx - step_idx) % cp_size
            cur_state = block_update(cur_state, queries, k_cur, v_cur, src_idx < my_idx)
            return cur_state, k_cur, v_cur

        sm_state, k_last, v_last = lax.fori_loop(1, cp_size, kv_step, (sm_state, k_rot, values))
        return finish(sm_state, hidden, w_o)

    rep_spec = P(None, None, None)
    return jax.shard_map(per_device, mesh=mesh, in_specs=(P('dp', 'cp', None), P('dp', 'cp'), rep_spec, rep_spec, rep_spec, rep_spec), out_specs=P('dp', 'cp', None), check_vma=False)
```

profile of v0, /device:TPU:6, one launch (start us, length us, event | category | flops | bytes accessed | tf_op | source)
XLA Modules:
  0.0 3063.4 jit_solution(3010034938844323920)
XLA Ops:
  0.0 54.8 %copy.9 = bf16[5120,32,128]{0,2,1:T(8,128)(2,1)} copy(bf16[5120,32,128]{2,1,0:T(8,128)(2,1)} %param.10) | data formatting | bytes 83886080 | tf_op args[2]
  54.8 185.2 %convert_convert_fusion = f32[16,256,32,128]{1,3,2,0:T(8,128)} fusion(bf16[5120,32,128]{0,2,1:T(8,128)(2,1)} %copy.9, bf16[16,256,5120]{2,1,0:T(8,128)(2,1)} %param.8), kind=kOutput, calls=%fused_computation.45 | convolution fusion | flops 171832246272 | bytes 150994944 | tf_op jit(solution)/shard_map/bsd,dhe->bshe/dot_general | solution.py:27
  240.0 43.2 %slice_negate_fusion = (f32[16,256,32,64]{1,3,2,0:T(8,128)}, f32[16,256,32,64]{1,3,2,0:T(8,128)}) fusion(f32[16,256,32,128]{1,3,2,0:T(8,128)} %convert_convert_fusion), kind=kLoop, calls=%fused_computation.42 | loop fusion | flops 8388608 | bytes 134217728 | tf_op jit(solution)/shard_map/neg | solution.py:19
  283.4 7.3 fusion.60
  290.7 53.6 %fusion.23 = bf16[16,256,32,128]{1,3,2,0:T(8,128)(2,1)} fusion(f32[16,256,32,64]{1,3,2,0:T(8,128)} %get-tuple-element.236, f32[16,256,32,64]{1,3,2,0:T(8,128)} %get-tuple-element.235, f32[16,256,32,128]{1,3,2,0:T(8,128)} %convert_convert_fusion, f32[16,256,128]{1,2,0:T(8,128)S(1)} %get-tuple-element.240, f32[16,256,128]{1,2,0:T(8,128)S(1)} %get-tuple-element.239), kind=kLoop, calls=%fused_computation.29 | loop fusion | flops 83886080 | bytes 171966464 | tf_op jit(solution)/shard_map/convert_element_type | solution.py:20
  344.3 14.4 copy.8
  358.7 53.1 %convert_convert_fusion.1 = f32[16,256,8,128]{1,3,2,0:T(8,128)} fusion(bf16[5120,8,128]{0,2,1:T(8,128)(2,1)} %copy.8, bf16[16,256,5120]{2,1,0:T(8,128)(2,1)} %param.8), kind=kOutput, calls=%fused_computation.56 | convolution fusion | flops 42958061568 | bytes 69206016 | tf_op jit(solution)/shard_map/bsd,dhe->bshe/dot_general | solution.py:28
  411.8 13.2 slice_negate_fusion.1
  425.1 3.1 copy-done
  428.2 10.6 fusion.43
  438.8 61.5 %fusion.18 = (f32[16,8,4,256]{3,2,1,0:T(4,128)}, f32[16,8,256,256,4]{3,2,4,1,0:T(8,128)}) fusion(pred[256,256]{0,1:T(8,128)(4,1)S(1)} %iota_compare_fusion, bf16[16,256,8,4,128]{1,4,3,2,0:T(8,128)(2,1)} %bitcast.135, bf16[16,256,8,128]{1,3,2,0:T(8,128)(2,1)} %fusion.43), kind=kOutput, calls=%fused_computation.23 | convolution fusion | flops 8690466816 | bytes 176750592 | tf_op jit(solution)/shard_map/bqkge,bske->bkgqs/dot_general | solution.py:47
  500.3 41.4 %fusion.17 = f32[16,8,4,256]{3,2,1,0:T(4,128)S(1)} fusion(f32[16,8,256,256,4]{3,2,4,1,0:T(8,128)} %get-tuple-element.244, f32[16,8,4,256]{3,2,1,0:T(4,128)} %get-tuple-element.307, pred[256,256]{0,1:T(8,128)(4,1)S(1)} %iota_compare_fusion), kind=kLoop, calls=%fused_computation.22 | loop fusion | flops 134086656 | bytes 135331840 | tf_op jit(solution)/shard_map/reduce_sum | solution.py:52
  543.9 50.2 %fusion.54 = bf16[16,256,8,128]{3,1,2,0:T(8,128)(2,1)S(1)} fusion(bf16[5120,8,128]{2,1,0:T(8,128)(2,1)} %param.12, bf16[16,256,5120]{2,1,0:T(8,128)(2,1)} %param.8), kind=kOutput, calls=%fused_computation.57 | convolution fusion | flops 42953867264 | bytes 60817408 | tf_op jit(solution)/shard_map/bsd,dhe->bshe/dot_general | solution.py:29
  594.1 81.2 %broadcast_add_fusion = f32[16,8,4,256,128]{4,3,2,1,0:T(8,128)} fusion(f32[16,8,4,256]{3,2,1,0:T(4,128)S(1)} %get-tuple-element.241, f32[16,8,256,256,4]{3,2,4,1,0:T(8,128)} %get-tuple-element.244, f32[16,8,4,256]{3,2,1,0:T(4,128)} %get-tuple-element.307, pred[256,256]{0,1:T(8,128)(4,1)S(1)} %iota_compare_fusion, bf16[16,256,8,128]{3,1,2,0:T(8,128)(2,1)S(1)} %fusion.54), kind=kOutput, calls=%fused_computation.44 | convolution fusion | flops 8740929536 | bytes 210829312 | tf_op jit(solution)/shard_map/bkgqs,bske->bkgqe/dot_general | solution.py:53
  675.3 42.0 %copy.15 = bf16[16,256,8,4,128]{4,1,3,2,0:T(8,128)(2,1)} copy(bf16[16,256,8,4,128]{1,4,3,2,0:T(8,128)(2,1)} %bitcast.136) | data formatting | bytes 67108864 | tf_op jit(solution)/shard_map/while | solution.py:87
  717.3 12.3 copy.14
  729.7 2108.5 %while.23 = (s32[]{:T(128)}, f32[16,8,4,256]{3,2,1,0:T(4,128)}, f32[16,8,4,256]{3,2,1,0:T(4,128)S(1)}, f32[16,8,4,256,128]{4,3,2,1,0:T(8,128)}, bf16[16,256,8,12...) while((s32[]{:T(128)}, f32[16,8,4,256]{3,2,1,0:T(4,128)}, ...), condition=%wide.region_5.6_spmd, body=%wide.region_2.5_spmd.sunk | while | flops 17582784512 | bytes 696254848 | solution.py:87
  729.7 92.8 %collective-permute-done = bf16[16,256,8,128]{3,1,2,0:T(8,128)(2,1)} collective-permute-done((bf16[16,256,8,128]{3,1,2,0:T(8,128)(2,1)}, bf16[16,256,8,128]{3,1,2,0:T(8,128)(2,1)}, u32[]{:S(2)}, u32[]{:S(2)}) %collective-permute-start) | collective-permute-done | bytes 8388640 | tf_op jit(solution)/shard_map/while/body/eval_jaxpr/ppermute | solution.py:81
  822.5 59.9 %bitcast_reduce_fusion.2 = (f32[16,8,4,256]{3,2,1,0:T(4,128)S(1)}, f32[16,8,256,256,4]{3,2,4,1,0:T(8,128)}) fusion(pred[]{:T(512)S(6)} %lt.31, bf16[16,256,8,4,128]{4,1,3,2,0:T(8,128)(2,1)} %get-tuple-element.337, bf16[16,256,8,128]{3,1,2,0:T(8,128)(2,1)} %collective-permute-done), kind=kOutput, calls=%fused_computation.1.clone.1 | convolution fusion | flops 8690466816 | bytes 176685056 | tf_op jit(solution)/shard_map/while/body/eval_jaxpr/bqkge,bske->bkgqs/dot_general | solution.py:47
  883.7 41.2 %fusion.81 = f32[16,8,4,256]{3,2,1,0:T(4,128)S(1)} fusion(f32[16,8,256,256,4]{3,2,4,1,0:T(8,128)} %get-tuple-element.303, f32[16,8,4,256]{3,2,1,0:T(4,128)S(1)} %max.11, pred[]{:T(512)S(6)} %lt.31), kind=kLoop, calls=%fused_computation.5.clone.1 | loop fusion | flops 134086656 | bytes 135266304 | tf_op jit(solution)/shard_map/while/body/eval_jaxpr/reduce_sum | solution.py:52
  927.2 7.8 copy.56
  935.0 7.8 copy.57
  942.8 88.1 %multiply_add_fusion.5 = f32[16,8,4,256,128]{4,3,2,1,0:T(8,128)} fusion(f32[16,8,4,256,128]{4,3,2,1,0:T(8,128)} %get-tuple-element.321, f32[16,8,4,256]{3,2,1,0:T(4,128)S(1)} %bitcast.137, f32[16,8,256,256,4]{3,2,4,1,0:T(8,128)} %get-tuple-element.303, f32[16,8,4,256]{3,2,1,0:T(4,128)S(1)} %max.11, pred[]{:T(512)S(6)} %lt.31, ...), kind=kOutput, calls=%fused_computation.7.clone.2 | convolution fusion | flops 8757706752 | bytes 277872640 | tf_op jit(solution)/shard_map/while/body/eval_jaxpr/bkgqs,bske->bkgqe/dot_general | solution.py:53
  1031.6 92.2 %collective-permute-done = bf16[16,256,8,128]{3,1,2,0:T(8,128)(2,1)} collective-permute-done((bf16[16,256,8,128]{3,1,2,0:T(8,128)(2,1)}, bf16[16,256,8,128]{3,1,2,0:T(8,128)(2,1)}, u32[]{:S(2)}, u32[]{:S(2)}) %collective-permute-start) | collective-permute-done | bytes 8388640 | tf_op jit(solution)/shard_map/while/body/eval_jaxpr/ppermute | solution.py:81
  1123.8 59.9 %bitcast_reduce_fusion.2 = (f32[16,8,4,256]{3,2,1,0:T(4,128)S(1)}, f32[16,8,256,256,4]{3,2,4,1,0:T(8,128)}) fusion(pred[]{:T(512)S(6)} %lt.31, bf16[16,256,8,4,128]{4,1,3,2,0:T(8,128)(2,1)} %get-tuple-element.337, bf16[16,256,8,128]{3,1,2,0:T(8,128)(2,1)} %collective-permute-done), kind=kOutput, calls=%fused_computation.1.clone.1 | convolution fusion | flops 8690466816 | bytes 176685056 | tf_op jit(solution)/shard_map/while/body/eval_jaxpr/bqkge,bske->bkgqs/dot_general | solution.py:47
  1184.9 41.2 %fusion.81 = f32[16,8,4,256]{3,2,1,0:T(4,128)S(1)} fusion(f32[16,8,256,256,4]{3,2,4,1,0:T(8,128)} %get-tuple-element.303, f32[16,8,4,256]{3,2,1,0:T(4,128)S(1)} %max.11, pred[]{:T(512)S(6)} %lt.31), kind=kLoop, calls=%fused_computation.5.clone.1 | loop fusion | flops 134086656 | bytes 135266304 | tf_op jit(solution)/shard_map/while/body/eval_jaxpr/reduce_sum | solution.py:52
  1228.4 7.8 copy.56
  1236.2 7.8 copy.57
  1244.0 88.1 %multiply_add_fusion.5 = f32[16,8,4,256,128]{4,3,2,1,0:T(8,128)} fusion(f32[16,8,4,256,128]{4,3,2,1,0:T(8,128)} %get-tuple-element.321, f32[16,8,4,256]{3,2,1,0:T(4,128)S(1)} %bitcast.137, f32[16,8,256,256,4]{3,2,4,1,0:T(8,128)} %get-tuple-element.303, f32[16,8,4,256]{3,2,1,0:T(4,128)S(1)} %max.11, pred[]{:T(512)S(6)} %lt.31, ...), kind=kOutput, calls=%fused_computation.7.clone.2 | convolution fusion | flops 8757706752 | bytes 277872640 | tf_op jit(solution)/shard_map/while/body/eval_jaxpr/bkgqs,bske->bkgqe/dot_general | solution.py:53
  1333.7 91.3 %collective-permute-done = bf16[16,256,8,128]{3,1,2,0:T(8,128)(2,1)} collective-permute-done((bf16[16,256,8,128]{3,1,2,0:T(8,128)(2,1)}, bf16[16,256,8,128]{3,1,2,0:T(8,128)(2,1)}, u32[]{:S(2)}, u32[]{:S(2)}) %collective-permute-start) | collective-permute-done | bytes 8388640 | tf_op jit(solution)/shard_map/while/body/eval_jaxpr/ppermute | solution.py:81
  1425.0 59.9 %bitcast_reduce_fusion.2 = (f32[16,8,4,256]{3,2,1,0:T(4,128)S(1)}, f32[16,8,256,256,4]{3,2,4,1,0:T(8,128)}) fusion(pred[]{:T(512)S(6)} %lt.31, bf16[16,256,8,4,128]{4,1,3,2,0:T(8,128)(2,1)} %get-tuple-element.337, bf16[16,256,8,128]{3,1,2,0:T(8,128)(2,1)} %collective-permute-done), kind=kOutput, calls=%fused_computation.1.clone.1 | convolution fusion | flops 8690466816 | bytes 176685056 | tf_op jit(solution)/shard_map/while/body/eval_jaxpr/bqkge,bske->bkgqs/dot_general | solution.py:47
  1486.1 41.2 %fusion.81 = f32[16,8,4,256]{3,2,1,0:T(4,128)S(1)} fusion(f32[16,8,256,256,4]{3,2,4,1,0:T(8,128)} %get-tuple-element.303, f32[16,8,4,256]{3,2,1,0:T(4,128)S(1)} %max.11, pred[]{:T(512)S(6)} %lt.31), kind=kLoop, calls=%fused_computation.5.clone.1 | loop fusion | flops 134086656 | bytes 135266304 | tf_op jit(solution)/shard_map/while/body/eval_jaxpr/reduce_sum | solution.py:52
  1529.6 7.8 copy.56
  1537.4 7.8 copy.57
  1545.2 88.1 %multiply_add_fusion.5 = f32[16,8,4,256,128]{4,3,2,1,0:T(8,128)} fusion(f32[16,8,4,256,128]{4,3,2,1,0:T(8,128)} %get-tuple-element.321, f32[16,8,4,256]{3,2,1,0:T(4,128)S(1)} %bitcast.137, f32[16,8,256,256,4]{3,2,4,1,0:T(8,128)} %get-tuple-element.303, f32[16,8,4,256]{3,2,1,0:T(4,128)S(1)} %max.11, pred[]{:T(512)S(6)} %lt.31, ...), kind=kOutput, calls=%fused_computation.7.clone.2 | convolution fusion | flops 8757706752 | bytes 277872640 | tf_op jit(solution)/shard_map/while/body/eval_jaxpr/bkgqs,bske->bkgqe/dot_general | solution.py:53
  1633.3 2.5 collective-permute-start.1
  1635.8 90.3 %collective-permute-done = bf16[16,256,8,128]{3,1,2,0:T(8,128)(2,1)} collective-permute-done((bf16[16,256,8,128]{3,1,2,0:T(8,128)(2,1)}, bf16[16,256,8,128]{3,1,2,0:T(8,128)(2,1)}, u32[]{:S(2)}, u32[]{:S(2)}) %collective-permute-start) | collective-permute-done | bytes 8388640 | tf_op jit(solution)/shard_map/while/body/eval_jaxpr/ppermute | solution.py:81
  1726.2 59.9 %bitcast_reduce_fusion.2 = (f32[16,8,4,256]{3,2,1,0:T(4,128)S(1)}, f32[16,8,256,256,4]{3,2,4,1,0:T(8,128)}) fusion(pred[]{:T(512)S(6)} %lt.31, bf16[16,256,8,4,128]{4,1,3,2,0:T(8,128)(2,1)} %get-tuple-element.337, bf16[16,256,8,128]{3,1,2,0:T(8,128)(2,1)} %collective-permute-done), kind=kOutput, calls=%fused_computation.1.clone.1 | convolution fusion | flops 8690466816 | bytes 176685056 | tf_op jit(solution)/shard_map/while/body/eval_jaxpr/bqkge,bske->bkgqs/dot_general | solution.py:47
  1787.3 41.2 %fusion.81 = f32[16,8,4,256]{3,2,1,0:T(4,128)S(1)} fusion(f32[16,8,256,256,4]{3,2,4,1,0:T(8,128)} %get-tuple-element.303, f32[16,8,4,256]{3,2,1,0:T(4,128)S(1)} %max.11, pred[]{:T(512)S(6)} %lt.31), kind=kLoop, calls=%fused_computation.5.clone.1 | loop fusion | flops 134086656 | bytes 135266304 | tf_op jit(solution)/shard_map/while/body/eval_jaxpr/reduce_sum | solution.py:52
  1830.8 7.8 copy.56
  1838.6 7.8 copy.57
  1846.4 88.1 %multiply_add_fusion.5 = f32[16,8,4,256,128]{4,3,2,1,0:T(8,128)} fusion(f32[16,8,4,256,128]{4,3,2,1,0:T(8,128)} %get-tuple-element.321, f32[16,8,4,256]{3,2,1,0:T(4,128)S(1)} %bitcast.137, f32[16,8,256,256,4]{3,2,4,1,0:T(8,128)} %get-tuple-element.303, f32[16,8,4,256]{3,2,1,0:T(4,128)S(1)} %max.11, pred[]{:T(512)S(6)} %lt.31, ...), kind=kOutput, calls=%fused_computation.7.clone.2 | convolution fusion | flops 8757706752 | bytes 277872640 | tf_op jit(solution)/shard_map/while/body/eval_jaxpr/bkgqs,bske->bkgqe/dot_general | solution.py:53
  1934.5 3.4 collective-permute-start.1
  1937.9 89.4 %collective-permute-done = bf16[16,256,8,128]{3,1,2,0:T(8,128)(2,1)} collective-permute-done((bf16[16,256,8,128]{3,1,2,0:T(8,128)(2,1)}, bf16[16,256,8,128]{3,1,2,0:T(8,128)(2,1)}, u32[]{:S(2)}, u32[]{:S(2)}) %collective-permute-start) | collective-permute-done | bytes 8388640 | tf_op jit(solution)/shard_map/while/body/eval_jaxpr/ppermute | solution.py:81
  2027.4 59.9 %bitcast_reduce_fusion.2 = (f32[16,8,4,256]{3,2,1,0:T(4,128)S(1)}, f32[16,8,256,256,4]{3,2,4,1,0:T(8,128)}) fusion(pred[]{:T(512)S(6)} %lt.31, bf16[16,256,8,4,128]{4,1,3,2,0:T(8,128)(2,1)} %get-tuple-element.337, bf16[16,256,8,128]{3,1,2,0:T(8,128)(2,1)} %collective-permute-done), kind=kOutput, calls=%fused_computation.1.clone.1 | convolution fusion | flops 8690466816 | bytes 176685056 | tf_op jit(solution)/shard_map/while/body/eval_jaxpr/bqkge,bske->bkgqs/dot_general | solution.py:47
  2088.5 41.2 %fusion.81 = f32[16,8,4,256]{3,2,1,0:T(4,128)S(1)} fusion(f32[16,8,256,256,4]{3,2,4,1,0:T(8,128)} %get-tuple-element.303, f32[16,8,4,256]{3,2,1,0:T(4,128)S(1)} %max.11, pred[]{:T(512)S(6)} %lt.31), kind=kLoop, calls=%fused_computation.5.clone.1 | loop fusion | flops 134086656 | bytes 135266304 | tf_op jit(solution)/shard_map/while/body/eval_jaxpr/reduce_sum | solution.py:52
  2132.1 7.8 copy.56
  2139.8 7.8 copy.57
  2147.6 88.1 %multiply_add_fusion.5 = f32[16,8,4,256,128]{4,3,2,1,0:T(8,128)} fusion(f32[16,8,4,256,128]{4,3,2,1,0:T(8,128)} %get-tuple-element.321, f32[16,8,4,256]{3,2,1,0:T(4,128)S(1)} %bitcast.137, f32[16,8,256,256,4]{3,2,4,1,0:T(8,128)} %get-tuple-element.303, f32[16,8,4,256]{3,2,1,0:T(4,128)S(1)} %max.11, pred[]{:T(512)S(6)} %lt.31, ...), kind=kOutput, calls=%fused_computation.7.clone.2 | convolution fusion | flops 8757706752 | bytes 277872640 | tf_op jit(solution)/shard_map/while/body/eval_jaxpr/bkgqs,bske->bkgqe/dot_general | solution.py:53
  2236.7 3.4 collective-permute-start.1
  2240.1 88.5 %collective-permute-done = bf16[16,256,8,128]{3,1,2,0:T(8,128)(2,1)} collective-permute-done((bf16[16,256,8,128]{3,1,2,0:T(8,128)(2,1)}, bf16[16,256,8,128]{3,1,2,0:T(8,128)(2,1)}, u32[]{:S(2)}, u32[]{:S(2)}) %collective-permute-start) | collective-permute-done | bytes 8388640 | tf_op jit(solution)/shard_map/while/body/eval_jaxpr/ppermute | solution.py:81
  2328.6 59.9 %bitcast_reduce_fusion.2 = (f32[16,8,4,256]{3,2,1,0:T(4,128)S(1)}, f32[16,8,256,256,4]{3,2,4,1,0:T(8,128)}) fusion(pred[]{:T(512)S(6)} %lt.31, bf16[16,256,8,4,128]{4,1,3,2,0:T(8,128)(2,1)} %get-tuple-element.337, bf16[16,256,8,128]{3,1,2,0:T(8,128)(2,1)} %collective-permute-done), kind=kOutput, calls=%fused_computation.1.clone.1 | convolution fusion | flops 8690466816 | bytes 176685056 | tf_op jit(solution)/shard_map/while/body/eval_jaxpr/bqkge,bske->bkgqs/dot_general | solution.py:47
  2389.7 41.2 %fusion.81 = f32[16,8,4,256]{3,2,1,0:T(4,128)S(1)} fusion(f32[16,8,256,256,4]{3,2,4,1,0:T(8,128)} %get-tuple-element.303, f32[16,8,4,256]{3,2,1,0:T(4,128)S(1)} %max.11, pred[]{:T(512)S(6)} %lt.31), kind=kLoop, calls=%fused_computation.5.clone.1 | loop fusion | flops 134086656 | bytes 135266304 | tf_op jit(solution)/shard_map/while/body/eval_jaxpr/reduce_sum | solution.py:52
  2433.3 7.8 copy.56
  2441.1 7.8 copy.57
  2448.9 88.1 %multiply_add_fusion.5 = f32[16,8,4,256,128]{4,3,2,1,0:T(8,128)} fusion(f32[16,8,4,256,128]{4,3,2,1,0:T(8,128)} %get-tuple-element.321, f32[16,8,4,256]{3,2,1,0:T(4,128)S(1)} %bitcast.137, f32[16,8,256,256,4]{3,2,4,1,0:T(8,128)} %get-tuple-element.303, f32[16,8,4,256]{3,2,1,0:T(4,128)S(1)} %max.11, pred[]{:T(512)S(6)} %lt.31, ...), kind=kOutput, calls=%fused_computation.7.clone.2 | convolution fusion | flops 8757706752 | bytes 277872640 | tf_op jit(solution)/shard_map/while/body/eval_jaxpr/bkgqs,bske->bkgqe/dot_general | solution.py:53
  2538.8 3.4 collective-permute-start.1
  2542.2 87.6 %collective-permute-done = bf16[16,256,8,128]{3,1,2,0:T(8,128)(2,1)} collective-permute-done((bf16[16,256,8,128]{3,1,2,0:T(8,128)(2,1)}, bf16[16,256,8,128]{3,1,2,0:T(8,128)(2,1)}, u32[]{:S(2)}, u32[]{:S(2)}) %collective-permute-start) | collective-permute-done | bytes 8388640 | tf_op jit(solution)/shard_map/while/body/eval_jaxpr/ppermute | solution.py:81
  2629.8 59.9 %bitcast_reduce_fusion.2 = (f32[16,8,4,256]{3,2,1,0:T(4,128)S(1)}, f32[16,8,256,256,4]{3,2,4,1,0:T(8,128)}) fusion(pred[]{:T(512)S(6)} %lt.31, bf16[16,256,8,4,128]{4,1,3,2,0:T(8,128)(2,1)} %get-tuple-element.337, bf16[16,256,8,128]{3,1,2,0:T(8,128)(2,1)} %collective-permute-done), kind=kOutput, calls=%fused_computation.1.clone.1 | convolution fusion | flops 8690466816 | bytes 176685056 | tf_op jit(solution)/shard_map/while/body/eval_jaxpr/bqkge,bske->bkgqs/dot_general | solution.py:47
  2690.9 41.2 %fusion.81 = f32[16,8,4,256]{3,2,1,0:T(4,128)S(1)} fusion(f32[16,8,256,256,4]{3,2,4,1,0:T(8,128)} %get-tuple-element.303, f32[16,8,4,256]{3,2,1,0:T(4,128)S(1)} %max.11, pred[]{:T(512)S(6)} %lt.31), kind=kLoop, calls=%fused_computation.5.clone.1 | loop fusion | flops 134086656 | bytes 135266304 | tf_op jit(solution)/shard_map/while/body/eval_jaxpr/reduce_sum | solution.py:52
  2734.5 7.8 copy.56
  2742.3 7.8 copy.57
  2750.1 88.1 %multiply_add_fusion.5 = f32[16,8,4,256,128]{4,3,2,1,0:T(8,128)} fusion(f32[16,8,4,256,128]{4,3,2,1,0:T(8,128)} %get-tuple-element.321, f32[16,8,4,256]{3,2,1,0:T(4,128)S(1)} %bitcast.137, f32[16,8,256,256,4]{3,2,4,1,0:T(8,128)} %get-tuple-element.303, f32[16,8,4,256]{3,2,1,0:T(4,128)S(1)} %max.11, pred[]{:T(512)S(6)} %lt.31, ...), kind=kOutput, calls=%fused_computation.7.clone.2 | convolution fusion | flops 8757706752 | bytes 277872640 | tf_op jit(solution)/shard_map/while/body/eval_jaxpr/bkgqs,bske->bkgqe/dot_general | solution.py:53
  2838.2 224.8 %fusion.19 = bf16[16,256,5120]{2,1,0:T(8,128)(2,1)} fusion(bf16[16,256,5120]{2,1,0:T(8,128)(2,1)} %param.8, bf16[8,4,128,5120,1]{3,2,1,0,4:T(8,128)(2,1)} %bitcast.141, f32[16,8,4,256,128]{4,3,2,1,0:T(8,128)} %get-tuple-element.205, f32[16,8,4,256]{3,2,1,0:T(4,128)S(1)} %get-tuple-element.206), kind=kOutput, calls=%fused_computation.25 | convolution fusion | flops 171895160832 | bytes 193462272 | tf_op jit(solution)/shard_map/clhrf,lhfe->cre/dot_general | solution.py:63
  (54 shorter events, 31.9 us)
Async XLA Ops:
  240.0 43.2 %copy-start.4 = (s32[16,256]{1,0:T(8,128)S(1)}, s32[16,256]{1,0:T(8,128)}, u32[]{:S(2)}) copy-start(s32[16,256]{1,0:T(8,128)} %param.9) | copy-start | bytes 49156
  290.7 53.7 %copy-start.1 = (f32[16,256,128]{1,2,0:T(8,128)}, f32[16,256,128]{1,2,0:T(8,128)S(1)}, u32[]{:S(2)}) copy-start(f32[16,256,128]{1,2,0:T(8,128)S(1)} %get-tuple-element.240) | copy-start | bytes 6291460
  358.7 66.4 %copy-start.2 = (f32[16,256,128]{1,2,0:T(8,128)S(1)}, f32[16,256,128]{1,2,0:T(8,128)}, u32[]{:S(2)}) copy-start(f32[16,256,128]{1,2,0:T(8,128)} %copy-done.1) | copy-start | bytes 6291460
  411.8 16.3 copy-start
  594.1 81.2 %copy-start.5 = (bf16[16,256,8,128]{3,1,2,0:T(8,128)(2,1)}, bf16[16,256,8,128]{3,1,2,0:T(8,128)(2,1)S(1)}, u32[]{:S(2)}) copy-start(bf16[16,256,8,128]{3,1,2,0:T(8,128)(2,1)S(1)} %fusion.54) | copy-start | bytes 25165828
  675.3 54.4 %copy-start.3 = (f32[16,8,4,256]{3,2,1,0:T(4,128)S(1)}, f32[16,8,4,256]{3,2,1,0:T(4,128)}, u32[]{:S(2)}) copy-start(f32[16,8,4,256]{3,2,1,0:T(4,128)} %get-tuple-element.308) | copy-start | bytes 1572868
  729.7 92.9 %collective-permute-start = (bf16[16,256,8,128]{3,1,2,0:T(8,128)(2,1)}, bf16[16,256,8,128]{3,1,2,0:T(8,128)(2,1)}, u32[]{:S(2)}, u32[]{:S(2)}) collective-permute-start(bf16[16,256,8,128]{3,1,2,0:T(8,128)(2,1)} %get-tuple-element.322), channel_id=1, source_target_pairs={{0,1},{1,2},{2,3},{3,4},{4,5},{5,6},{6,7},{7,0}} | collective-permute-start | bytes 25165832 | tf_op jit(solution)/shard_map/while/body/eval_jaxpr/ppermute | solution.py:81
  729.7 205.3 %collective-permute-start.1 = (bf16[16,256,8,128]{3,1,2,0:T(8,128)(2,1)}, bf16[16,256,8,128]{3,1,2,0:T(8,128)(2,1)}, u32[]{:S(2)}, u32[]{:S(2)}) collective-permute-start(bf16[16,256,8,128]{3,1,2,0:T(8,128)(2,1)} %get-tuple-element.323), channel_id=1, source_target_pairs={{0,1},{1,2},{2,3},{3,4},{4,5},{5,6},{6,7},{7,0}} | collective-permute-start | bytes 25165832 | tf_op jit(solution)/shard_map/while/body/eval_jaxpr/ppermute | solution.py:82
  1030.9 92.9 %collective-permute-start = (bf16[16,256,8,128]{3,1,2,0:T(8,128)(2,1)}, bf16[16,256,8,128]{3,1,2,0:T(8,128)(2,1)}, u32[]{:S(2)}, u32[]{:S(2)}) collective-permute-start(bf16[16,256,8,128]{3,1,2,0:T(8,128)(2,1)} %get-tuple-element.322), channel_id=1, source_target_pairs={{0,1},{1,2},{2,3},{3,4},{4,5},{5,6},{6,7},{7,0}} | collective-permute-start | bytes 25165832 | tf_op jit(solution)/shard_map/while/body/eval_jaxpr/ppermute | solution.py:81
  1030.9 205.3 %collective-permute-start.1 = (bf16[16,256,8,128]{3,1,2,0:T(8,128)(2,1)}, bf16[16,256,8,128]{3,1,2,0:T(8,128)(2,1)}, u32[]{:S(2)}, u32[]{:S(2)}) collective-permute-start(bf16[16,256,8,128]{3,1,2,0:T(8,128)(2,1)} %get-tuple-element.323), channel_id=1, source_target_pairs={{0,1},{1,2},{2,3},{3,4},{4,5},{5,6},{6,7},{7,0}} | collective-permute-start | bytes 25165832 | tf_op jit(solution)/shard_map/while/body/eval_jaxpr/ppermute | solution.py:82
  1332.1 92.9 %collective-permute-start = (bf16[16,256,8,128]{3,1,2,0:T(8,128)(2,1)}, bf16[16,256,8,128]{3,1,2,0:T(8,128)(2,1)}, u32[]{:S(2)}, u32[]{:S(2)}) collective-permute-start(bf16[16,256,8,128]{3,1,2,0:T(8,128)(2,1)} %get-tuple-element.322), channel_id=1, source_target_pairs={{0,1},{1,2},{2,3},{3,4},{4,5},{5,6},{6,7},{7,0}} | collective-permute-start | bytes 25165832 | tf_op jit(solution)/shard_map/while/body/eval_jaxpr/ppermute | solution.py:81
  1332.1 205.3 %collective-permute-start.1 = (bf16[16,256,8,128]{3,1,2,0:T(8,128)(2,1)}, bf16[16,256,8,128]{3,1,2,0:T(8,128)(2,1)}, u32[]{:S(2)}, u32[]{:S(2)}) collective-permute-start(bf16[16,256,8,128]{3,1,2,0:T(8,128)(2,1)} %get-tuple-element.323), channel_id=1, source_target_pairs={{0,1},{1,2},{2,3},{3,4},{4,5},{5,6},{6,7},{7,0}} | collective-permute-start | bytes 25165832 | tf_op jit(solution)/shard_map/while/body/eval_jaxpr/ppermute | solution.py:82
  1633.3 92.9 %collective-permute-start = (bf16[16,256,8,128]{3,1,2,0:T(8,128)(2,1)}, bf16[16,256,8,128]{3,1,2,0:T(8,128)(2,1)}, u32[]{:S(2)}, u32[]{:S(2)}) collective-permute-start(bf16[16,256,8,128]{3,1,2,0:T(8,128)(2,1)} %get-tuple-element.322), channel_id=1, source_target_pairs={{0,1},{1,2},{2,3},{3,4},{4,5},{5,6},{6,7},{7,0}} | collective-permute-start | bytes 25165832 | tf_op jit(solution)/shard_map/while/body/eval_jaxpr/ppermute | solution.py:81
  1633.3 205.3 %collective-permute-start.1 = (bf16[16,256,8,128]{3,1,2,0:T(8,128)(2,1)}, bf16[16,256,8,128]{3,1,2,0:T(8,128)(2,1)}, u32[]{:S(2)}, u32[]{:S(2)}) collective-permute-start(bf16[16,256,8,128]{3,1,2,0:T(8,128)(2,1)} %get-tuple-element.323), channel_id=1, source_target_pairs={{0,1},{1,2},{2,3},{3,4},{4,5},{5,6},{6,7},{7,0}} | collective-permute-start | bytes 25165832 | tf_op jit(solution)/shard_map/while/body/eval_jaxpr/ppermute | solution.py:82
  1934.5 92.9 %collective-permute-start = (bf16[16,256,8,128]{3,1,2,0:T(8,128)(2,1)}, bf16[16,256,8,128]{3,1,2,0:T(8,128)(2,1)}, u32[]{:S(2)}, u32[]{:S(2)}) collective-permute-start(bf16[16,256,8,128]{3,1,2,0:T(8,128)(2,1)} %get-tuple-element.322), channel_id=1, source_target_pairs={{0,1},{1,2},{2,3},{3,4},{4,5},{5,6},{6,7},{7,0}} | collective-permute-start | bytes 25165832 | tf_op jit(solution)/shard_map/while/body/eval_jaxpr/ppermute | solution.py:81
  1934.5 205.3 %collective-permute-start.1 = (bf16[16,256,8,128]{3,1,2,0:T(8,128)(2,1)}, bf16[16,256,8,128]{3,1,2,0:T(8,128)(2,1)}, u32[]{:S(2)}, u32[]{:S(2)}) collective-permute-start(bf16[16,256,8,128]{3,1,2,0:T(8,128)(2,1)} %get-tuple-element.323), channel_id=1, source_target_pairs={{0,1},{1,2},{2,3},{3,4},{4,5},{5,6},{6,7},{7,0}} | collective-permute-start | bytes 25165832 | tf_op jit(solution)/shard_map/while/body/eval_jaxpr/ppermute | solution.py:82
  2235.7 92.9 %collective-permute-start = (bf16[16,256,8,128]{3,1,2,0:T(8,128)(2,1)}, bf16[16,256,8,128]{3,1,2,0:T(8,128)(2,1)}, u32[]{:S(2)}, u32[]{:S(2)}) collective-permute-start(bf16[16,256,8,128]{3,1,2,0:T(8,128)(2,1)} %get-tuple-element.322), channel_id=1, source_target_pairs={{0,1},{1,2},{2,3},{3,4},{4,5},{5,6},{6,7},{7,0}} | collective-permute-start | bytes 25165832 | tf_op jit(solution)/shard_map/while/body/eval_jaxpr/ppermute | solution.py:81
  2236.7 204.4 %collective-permute-start.1 = (bf16[16,256,8,128]{3,1,2,0:T(8,128)(2,1)}, bf16[16,256,8,128]{3,1,2,0:T(8,128)(2,1)}, u32[]{:S(2)}, u32[]{:S(2)}) collective-permute-start(bf16[16,256,8,128]{3,1,2,0:T(8,128)(2,1)} %get-tuple-element.323), channel_id=1, source_target_pairs={{0,1},{1,2},{2,3},{3,4},{4,5},{5,6},{6,7},{7,0}} | collective-permute-start | bytes 25165832 | tf_op jit(solution)/shard_map/while/body/eval_jaxpr/ppermute | solution.py:82
  2536.9 92.9 %collective-permute-start = (bf16[16,256,8,128]{3,1,2,0:T(8,128)(2,1)}, bf16[16,256,8,128]{3,1,2,0:T(8,128)(2,1)}, u32[]{:S(2)}, u32[]{:S(2)}) collective-permute-start(bf16[16,256,8,128]{3,1,2,0:T(8,128)(2,1)} %get-tuple-element.322), channel_id=1, source_target_pairs={{0,1},{1,2},{2,3},{3,4},{4,5},{5,6},{6,7},{7,0}} | collective-permute-start | bytes 25165832 | tf_op jit(solution)/shard_map/while/body/eval_jaxpr/ppermute | solution.py:81
  2538.8 203.5 %collective-permute-start.1 = (bf16[16,256,8,128]{3,1,2,0:T(8,128)(2,1)}, bf16[16,256,8,128]{3,1,2,0:T(8,128)(2,1)}, u32[]{:S(2)}, u32[]{:S(2)}) collective-permute-start(bf16[16,256,8,128]{3,1,2,0:T(8,128)(2,1)} %get-tuple-element.323), channel_id=1, source_target_pairs={{0,1},{1,2},{2,3},{3,4},{4,5},{5,6},{6,7},{7,0}} | collective-permute-start | bytes 25165832 | tf_op jit(solution)/shard_map/while/body/eval_jaxpr/ppermute | solution.py:82
where the time goes:
time: 3080 us; the launch traced here: 3060 us
  matrix products  1690 us (55%)
  waiting for transfers between devices  632 us (21%)
  other arithmetic  479 us (16%)
  local copies, waits for them, and re-layouts  241 us (8%)
    dot_general x8, matrix products, block_update(): jnp.einsum('bkgqs,bske->bkgqe', p_weights.astype(jnp.bfloat16), v_blk, pr...  698 us
    ppermute x7, waiting for transfers between devices, kv_step(): k_cur = lax.ppermute(k_cur, 'cp', shift_pairs)  632 us
    dot_general x8, matrix products, block_update(): jnp.einsum('bqkge,bske->bkgqs', queries, k_blk, preferred_element_type=jn...  481 us
    reduce_sum x8, other arithmetic, block_update(): run_sum = run_sum * correction + jnp.sum(p_weights, axis=-1)  330 us
    dot_general x1, matrix products, finish(): jnp.einsum('clhrf,lhfe->cre', attn_out, w_o_grp, preferred_element_type=j...  225 us
    dot_general x1, matrix products, project_qkv(): jnp.einsum('bsd,dhe->bshe', hidden, w_q, preferred_element_type=jnp.float32)  185 us
    while x21, local copies, waits for them, and re-layouts  115 us
    unnamed x14, local copies, waits for them, and re-layouts  72.3 us
  transfers between devices with their start and end apart: 14, of which 7 were waited for; matrix products, arithmetic and copies ran while one was open for 26% of the time, Pallas kernels for 0%

commit v1 on v0

v1 whole, which is shorter than its diff:
```python
import functools

import jax
import jax.numpy as jnp
from jax import lax
from jax.experimental import pallas as pl
from jax.experimental.pallas import tpu as pltpu
from jax.sharding import PartitionSpec as P

ROPE_BASE = 500000.0
HEAD = 128
LOG2E = 1.4426950408889634
VMEM_LIMIT = 60 * 1024 * 1024
CHUNKS = (4, 4, 4, 4)


def rope_tables(positions):
    inv_freq = ROPE_BASE ** (-jnp.arange(0, HEAD, 2, dtype=jnp.float32) / HEAD)
    angles = positions.astype(jnp.float32).reshape(-1, 1) * inv_freq
    cos, sin = jnp.cos(angles), jnp.sin(angles)
    return jnp.concatenate([cos, cos], axis=-1), jnp.concatenate([-sin, sin], axis=-1)


def rope_round(vals, cos, sin):
    vals = vals.astype(jnp.bfloat16).astype(jnp.float32)
    return (vals * cos + pltpu.roll(vals, HEAD // 2, 1) * sin).astype(jnp.bfloat16)


def q_kernel(x_ref, w_ref, cos_ref, sin_ref, o_ref):
    rows, width = o_ref.shape
    step = 512

    @pl.loop(0, rows // step)
    def _(r):
        at = pl.ds(pl.multiple_of(r * step, step), step)
        x = x_ref[at, :]
        cos, sin = cos_ref[at, :], sin_ref[at, :]
        for c in range(0, width, 256):
            acc = jnp.dot(x, w_ref[:, c:c + 256], preferred_element_type=jnp.float32)
            o_ref[at, c:c + HEAD] = rope_round(acc[:, :HEAD], cos, sin)
            o_ref[at, c + HEAD:c + 256] = rope_round(acc[:, HEAD:], cos, sin)


def project_q(x, w, cos, sin, tile_m=1024, tile_n=512):
    m, d = x.shape
    n = w.shape[1]
    return pl.pallas_call(
        q_kernel,
        out_shape=jax.ShapeDtypeStruct((m, n), jnp.bfloat16),
        grid=(m // tile_m, n // tile_n),
        in_specs=[
            pl.BlockSpec((tile_m, d), lambda i, j: (i, 0)),
            pl.BlockSpec((d, tile_n), lambda i, j: (0, j)),
            pl.BlockSpec((tile_m, HEAD), lambda i, j: (i, 0)),
            pl.BlockSpec((tile_m, HEAD), lambda i, j: (i, 0)),
        ],
        out_specs=pl.BlockSpec((tile_m, tile_n), lambda i, j: (i, j)),
        compiler_params=pltpu.CompilerParams(vmem_limit_bytes=VMEM_LIMIT),
        cost_estimate=pl.CostEstimate(flops=2 * m * n * d, bytes_accessed=2 * (m * d + m * n + 4 * n * d), transcendentals=0),
        name="project_q",
    )(x, w, cos, sin)


def kv_kernel(x_ref, wk_ref, wv_ref, cos_ref, sin_ref, k_ref, v_ref):
    seqs, tok = v_ref.shape[0], v_ref.shape[2]

    @pl.loop(0, seqs)
    def _(s):
        at = pl.ds(pl.multiple_of(s * tok, tok), tok)
        x = x_ref[at, :]
        cos, sin = cos_ref[at, :], sin_ref[at, :]
        for c in range(0, wk_ref.shape[1], 256):
            acc = jnp.dot(x, wk_ref[:, c:c + 256], preferred_element_type=jnp.float32)
            k_ref[s, :, c:c + HEAD] = rope_round(acc[:, :HEAD], cos, sin)
            k_ref[s, :, c + HEAD:c + 256] = rope_round(acc[:, HEAD:], cos, sin)
            acc = jnp.dot(x, wv_ref[:, c:c + 256], preferred_element_type=jnp.float32)
            v_ref[s, c:c + 256, :] = acc.T.astype(jnp.bfloat16)


def project_kv(x, w_k, w_v, cos, sin, seq0, seqs, tok, tile_n=256):
    d, n = w_k.shape
    rows = seqs * tok
    assert seq0 % seqs == 0
    i0 = seq0 // seqs
    return pl.pallas_call(
        kv_kernel,
        out_shape=(
            jax.ShapeDtypeStruct((seqs, tok, n), jnp.bfloat16),
            jax.ShapeDtypeStruct((seqs, n, tok), jnp.bfloat16),
        ),
        grid=(n // tile_n,),
        in_specs=[
            pl.BlockSpec((rows, d), lambda j: (i0, 0)),
            pl.BlockSpec((d, tile_n), lambda j: (0, j)),
            pl.BlockSpec((d, tile_n), lambda j: (0, j)),
            pl.BlockSpec((rows, HEAD), lambda j: (i0, 0)),
            pl.BlockSpec((rows, HEAD), lambda j: (i0, 0)),
        ],
        out_specs=(
            pl.BlockSpec((seqs, tok, tile_n), lambda j: (0, 0, j)),
            pl.BlockSpec((seqs, tile_n, tok), lambda j: (0, j, 0)),
        ),
        compiler_params=pltpu.CompilerParams(vmem_limit_bytes=VMEM_LIMIT),
        cost_estimate=pl.CostEstimate(flops=4 * rows * n * d, bytes_accessed=2 * rows * d + 4 * n * d + 4 * rows * n, transcendentals=0),
        name="project_kv",
    )(x, w_k, w_v, cos, sin)


def attn_kernel(me_ref, q_ref, k_ref, v_ref, *rest):
    o_ref, s_even, s_odd = rest[-3:]
    me = me_ref[0]
    tok = q_ref.shape[1]
    heads = q_ref.shape[2] // HEAD
    scale = HEAD ** -0.5 * LOG2E
    bufs = (s_even, s_odd)

    def scores(h, blocks, first_masked):
        buf = bufs[h % 2]
        q = q_ref[0, :, h * HEAD:(h + 1) * HEAD]
        top = jnp.full((8, tok), -jnp.inf, jnp.float32)
        for j in range(blocks):
            s = lax.dot_general(k_ref[j, 0], q, (((1,), (1,)), ((), ())), preferred_element_type=jnp.float32)
            if j >= first_masked:
                key = lax.broadcasted_iota(jnp.int32, (tok, tok), 0) + j * tok
                row = lax.broadcasted_iota(jnp.int32, (tok, tok), 1) + me * tok
                s = jnp.where(key <= row, s, -jnp.inf)
            buf[j * tok:(j + 1) * tok, :] = s
            top = jnp.maximum(top, jnp.max(s.reshape(tok // 8, 8, tok), axis=0))
        return jnp.max(top, axis=0, keepdims=True)

    def apply(h, blocks, top):
        buf = bufs[h % 2]
        shift = top * scale
        total = jnp.zeros((8, tok), jnp.float32)
        acc = None
        for j in range(blocks):
            p = jnp.exp2(buf[j * tok:(j + 1) * tok, :] * scale - shift)
            total = total + jnp.sum(p.reshape(tok // 8, 8, tok), axis=0)
            part = jnp.dot(v_ref[j, 0], p.astype(jnp.bfloat16), preferred_element_type=jnp.float32)
            acc = part if acc is None else acc + part
        out = acc * (1.0 / jnp.sum(total, axis=0, keepdims=True))
        o_ref[0, :, h * HEAD:(h + 1) * HEAD] = out.T.astype(jnp.bfloat16)

    def run(blocks, first_masked):
        tops = []
        for h in range(heads + 1):
            if h < heads:
                tops.append(scores(h, blocks, first_masked))
            if h > 0:
                apply(h - 1, blocks, tops[h - 1])

    n_dev = k_ref.shape[0]
    for pair in range(n_dev // 2):
        @pl.when(me // 2 == pair)
        def _():
            run(2 * pair + 2, 2 * pair)


def attention(me, q, k_all, v_all, seq0, after):
    n_dev, seqs, tok, kv_width = k_all.shape
    n_kv = kv_width // HEAD
    width = q.shape[2] // n_kv
    flops = 4 * seqs * tok * n_dev * tok * q.shape[2]
    return pl.pallas_call(
        attn_kernel,
        out_shape=jax.ShapeDtypeStruct((seqs, tok, q.shape[2]), jnp.bfloat16),
        grid_spec=pltpu.PrefetchScalarGridSpec(
            num_scalar_prefetch=1,
            grid=(seqs, n_kv),
            in_specs=[
                pl.BlockSpec((1, tok, width), lambda b, g, me: (b + seq0 if seq0 else b, 0, g)),
                pl.BlockSpec((n_dev, 1, tok, HEAD), lambda b, g, me: (0, b, 0, g)),
                pl.BlockSpec((n_dev, 1, HEAD, tok), lambda b, g, me: (0, b, g, 0)),
            ] + [pl.BlockSpec(memory_space=pl.ANY)] * len(after),
            out_specs=pl.BlockSpec((1, tok, width), lambda b, g, me: (b, 0, g)),
            scratch_shapes=[pltpu.VMEM((n_dev * tok, tok), jnp.float32)] * 2,
        ),
        compiler_params=pltpu.CompilerParams(vmem_limit_bytes=VMEM_LIMIT),
        cost_estimate=pl.CostEstimate(flops=flops, bytes_accessed=4 * k_all.size + 4 * seqs * tok * q.shape[2], transcendentals=0),
        name="attention",
    )(me, q, k_all, v_all, *after)


def o_kernel(o_ref, w_ref, x_ref, *rest):
    y_ref = rest[-1]
    rows = o_ref.shape[0]
    step = 512

    @pl.loop(0, rows // step)
    def _(r):
        at = pl.ds(pl.multiple_of(r * step, step), step)
        a = o_ref[at, :]
        for c in range(0, w_ref.shape[1], 256):
            acc = jnp.dot(a, w_ref[:, c:c + 256], preferred_element_type=jnp.float32)
            y_ref[at, c:c + 256] = (x_ref[at, c:c + 256].astype(jnp.float32) + acc).astype(jnp.bfloat16)


def project_o(o, w, x, y, row0, tile_n=512):
    rows, n_in = o.shape
    m, d = x.shape
    assert row0 % rows == 0
    i0 = row0 // rows
    specs = [
        pl.BlockSpec((rows, n_in), lambda j: (0, 0)),
        pl.BlockSpec((n_in, tile_n), lambda j: (0, j)),
        pl.BlockSpec((rows, tile_n), lambda j: (i0, j)),
    ]
    args = [o, w, x]
    alias = {}
    if y is not None:
        specs.append(pl.BlockSpec(memory_space=pl.ANY))
        args.append(y)
        alias = {3: 0}
    return pl.pallas_call(
        o_kernel,
        out_shape=jax.ShapeDtypeStruct((m, d), jnp.bfloat16),
        grid=(d // tile_n,),
        in_specs=specs,
        out_specs=pl.BlockSpec((rows, tile_n), lambda j: (i0, j)),
        input_output_aliases=alias,
        compiler_params=pltpu.CompilerParams(vmem_limit_bytes=VMEM_LIMIT),
        cost_estimate=pl.CostEstimate(flops=2 * rows * n_in * d, bytes_accessed=2 * (n_in * d + rows * n_in + 2 * rows * d), transcendentals=0),
        name="project_o",
    )(*args)


def solution(mesh):
    def per_device(hidden, positions, w_q, w_k, w_v, w_o):
        seqs, tok, d = hidden.shape
        x = hidden.reshape(seqs * tok, d)
        w_q = w_q.reshape(d, -1)
        w_k = w_k.reshape(d, -1)
        w_v = w_v.reshape(d, -1)
        w_o = w_o.reshape(-1, d)
        cos, sin = rope_tables(positions)
        me = lax.axis_index('cp').astype(jnp.int32).reshape(1)
        gathered = []
        seq0 = 0
        for n in CHUNKS:
            k, v = project_kv(x, w_k, w_v, cos, sin, seq0, n, tok)
            gathered.append((lax.all_gather(k, 'cp', axis=0), lax.all_gather(v, 'cp', axis=0)))
            seq0 += n
        q = project_q(x, w_q, cos, sin).reshape(seqs, tok, -1)
        y = None
        seq0 = 0
        for n, (k_all, v_all) in zip(CHUNKS, gathered):
            o = attention(me, q, k_all, v_all, seq0, () if y is None else (y,))
            y = project_o(o.reshape(n * tok, -1), w_o, x, y, seq0 * tok)
            seq0 += n
        return y.reshape(seqs, tok, d)

    rep_spec = P(None, None, None)
    return jax.shard_map(per_device, mesh=mesh, in_specs=(P('dp', 'cp', None), P('dp', 'cp'), rep_spec, rep_spec, rep_spec, rep_spec), out_specs=P('dp', 'cp', None), check_vma=False)
```

time: 3080 us -> 989 us (0.32)
  matrix products: 1690 us -> 0 us
  Pallas kernels: 0 us -> 899 us
  waiting for transfers between devices: 632 us -> 2.51 us
  other arithmetic: 479 us -> 11.4 us
  local copies, waits for them, and re-layouts: 241 us -> 49.6 us
    dot_general x20 -> x0, matrix products: 1690 us -> none  [the longest x8 698 us: block_update(): jnp.einsum('bkgqs,bske->bkgqe', p_weights.astype(jnp.bfloat16), v_blk, pr...]
    pallas_call x0 -> x13, Pallas kernels: none -> 899 us  [the longest x4 354 us: attention(): pl.pallas_call(attn_kernel, out_shape=jax.ShapeDtypeStruct((seqs, tok, q....]
    ppermute x14 -> x0, waiting for transfers between devices: 632 us -> none  [the longest x7 632 us: kv_step(): k_cur = lax.ppermute(k_cur, 'cp', shift_pairs)]
    reduce_sum x8 -> x0, other arithmetic: 330 us -> none  [block_update(): run_sum = run_sum * correction + jnp.sum(p_weights, axis=-1)]
    while x23 -> x0, local copies, waits for them, and re-layouts: 169 us -> none
    convert_element_type x3 -> x0, other arithmetic: 64.2 us -> none  [the longest x2 64.2 us: rope_apply(): return (val_f32 * cos_tab + rotated * sin_tab).astype(jnp.bfloat16)]
    neg x2 -> x1, other arithmetic: 56.4 us -> 7.48 us  [rope_tables(): -sin]
    unnamed x14 -> x2, local copies, waits for them, and re-layouts: 72.3 us -> 28.7 us
  transfers between devices with their start and end apart: 14 -> 8, of which waited for: 7 -> 0; matrix products, arithmetic and copies ran while one was open for 26% -> 3% of each run, Pallas kernels for 0% -> 74%
where the time goes in v1:
time: 989 us; the launch traced here: 977 us
  Pallas kernels  899 us (91%)
  local copies, waits for them, and re-layouts  49.6 us (5%)
  between operations  14 us (1%)
  other arithmetic  11.4 us (1%)
    pallas_call x4, Pallas kernels, attention(): pl.pallas_call(attn_kernel, out_shape=jax.ShapeDtypeStruct((seqs, tok, q....  354 us
    pallas_call x4, Pallas kernels, project_o(): pl.pallas_call(o_kernel, out_shape=jax.ShapeDtypeStruct((m, d), jnp.bfloa...  211 us
    pallas_call x1, Pallas kernels, project_q(): pl.pallas_call(q_kernel, out_shape=jax.ShapeDtypeStruct((m, n), jnp.bfloa...  201 us
    pallas_call x4, Pallas kernels, project_kv(): pl.pallas_call(kv_kernel, out_shape=(jax.ShapeDtypeStruct((seqs, tok, n),...  133 us
    unnamed x2, local copies, waits for them, and re-layouts  28.7 us
    reshape x1, local copies, waits for them, and re-layouts, per_device(): w_v = w_v.reshape(d, -1)  20.9 us
  transfers between devices with their start and end apart: 8, of which 0 were waited for; matrix products, arithmetic and copies ran while one was open for 3% of the time, Pallas kernels for 74%

profile of v1, /device:TPU:6, one launch (start us, length us, event | category | flops | bytes accessed | tf_op | source)
XLA Modules:
  0.0 977.0 jit_solution(13416641763011748561)
XLA Ops:
  6.5 0.0 all-gather.31.cloned.1.call-start
  6.5 0.7 convert_bitcast_fusion
  7.3 7.5 fusion
  14.8 20.9 %copy_bitcast_fusion.1 = (bf16[5120,1024]{1,0:T(8,128)(2,1)}, bf16[5120,1024]{1,0:T(8,128)(2,1)}) fusion(bf16[640,8,8,128]{3,2,1,0:T(8,128)(2,1)} %bitcast.45, bf16[640,8,8,128]{3,2,1,0:T(8,128)(2,1)} %bitcast.46), kind=kLoop, calls=%fused_computation.1 | loop fusion | bytes 41943040 | tf_op jit(solution)/shard_map/reshape | solution.py:233
  35.7 3.1 pad_maximum_fusion
  38.8 33.2 %project_kv.7 = (bf16[4,256,1024]{2,1,0:T(8,128)(2,1)}, bf16[4,1024,256]{2,1,0:T(8,128)(2,1)}) custom-call(bf16[4096,5120]{1,0:T(8,128)(2,1)} %bitcast.30, bf16[5120,1024]{1,0:T(8,128)(2,1)} %get-tuple-element.27.wk_ref, bf16[5120,1024]{1,0:T(8,128)(2,1)} %get-tuple-element.26.wv_ref, f32[4096,128]{1,0:T(8,128)} %get-tuple-element.24.cos_ref, ...), custom_call_target="tpu_custom_call" | custom-call | flops 21474836480 | bytes 35651584 | tf_op jit(solution)/shard_map/project_kv/pallas_call | solution.py:85
  72.0 0.0 all-gather.31.cloned.1.call-update
  72.0 0.0 all-gather.29.cloned.1.call-start
  72.1 0.7 all-gather.29.cloned.1.call-update
  72.8 0.0 all-gather.25.cloned.1.call-start
  72.8 33.2 %project_kv.6 = (bf16[4,256,1024]{2,1,0:T(8,128)(2,1)}, bf16[4,1024,256]{2,1,0:T(8,128)(2,1)}) custom-call(bf16[4096,5120]{1,0:T(8,128)(2,1)} %bitcast.31, bf16[5120,1024]{1,0:T(8,128)(2,1)} %get-tuple-element.27.wk_ref, bf16[5120,1024]{1,0:T(8,128)(2,1)} %get-tuple-element.26.wv_ref, f32[4096,128]{1,0:T(8,128)} %get-tuple-element.24.cos_ref, ...), custom_call_target="tpu_custom_call" | custom-call | flops 21474836480 | bytes 35651584 | tf_op jit(solution)/shard_map/project_kv/pallas_call | solution.py:85
  106.0 0.0 all-gather.25.cloned.1.call-update
  106.0 0.0 all-gather.27.cloned.1.call-start
  106.1 0.5 all-gather.27.cloned.1.call-update
  106.6 0.0 all-gather.21.cloned.1.call-start
  106.7 33.3 %project_kv.5 = (bf16[4,256,1024]{2,1,0:T(8,128)(2,1)}, bf16[4,1024,256]{2,1,0:T(8,128)(2,1)}) custom-call(bf16[4096,5120]{1,0:T(8,128)(2,1)} %bitcast.32, bf16[5120,1024]{1,0:T(8,128)(2,1)} %get-tuple-element.27.wk_ref, bf16[5120,1024]{1,0:T(8,128)(2,1)} %get-tuple-element.26.wv_ref, f32[4096,128]{1,0:T(8,128)} %get-tuple-element.24.cos_ref, ...), custom_call_target="tpu_custom_call" | custom-call | flops 21474836480 | bytes 35651584 | tf_op jit(solution)/shard_map/project_kv/pallas_call | solution.py:85
  139.9 0.0 all-gather.21.cloned.1.call-update
  140.0 0.0 all-gather.23.cloned.1.call-start
  140.0 0.5 all-gather.23.cloned.1.call-update
  140.6 0.2 all-gather.17.cloned.1.call-start
  140.8 33.2 %project_kv.4 = (bf16[4,256,1024]{2,1,0:T(8,128)(2,1)}, bf16[4,1024,256]{2,1,0:T(8,128)(2,1)}) custom-call(bf16[4096,5120]{1,0:T(8,128)(2,1)} %bitcast.33, bf16[5120,1024]{1,0:T(8,128)(2,1)} %get-tuple-element.27.wk_ref, bf16[5120,1024]{1,0:T(8,128)(2,1)} %get-tuple-element.26.wv_ref, f32[4096,128]{1,0:T(8,128)} %get-tuple-element.24.cos_ref, ...), custom_call_target="tpu_custom_call" | custom-call | flops 21474836480 | bytes 35651584 | tf_op jit(solution)/shard_map/project_kv/pallas_call | solution.py:85
  174.0 0.0 all-gather.17.cloned.1.call-update
  174.0 0.0 all-gather.19.cloned.1.call-start
  174.1 0.7 all-gather.19.cloned.1.call-update
  174.8 28.6 %copy.17 = bf16[640,8,32,128]{3,1,2,0:T(8,128)(2,1)} copy(bf16[640,8,32,128]{3,2,1,0:T(8,128)(2,1)} %bitcast.43) | data formatting | bytes 83886080
  203.4 201.0 %project_q.1 = bf16[4096,4096]{1,0:T(8,128)(2,1)} custom-call(bf16[4096,5120]{1,0:T(8,128)(2,1)} %bitcast.34, bf16[5120,4096]{1,0:T(8,128)(2,1)} %bitcast.44, f32[4096,128]{1,0:T(8,128)} %get-tuple-element.24.cos_ref, f32[4096,128]{1,0:T(8,128)} %get-tuple-element.25.sin_ref), custom_call_target="tpu_custom_call" | custom-call | flops 171798691840 | bytes 243269632 | tf_op jit(solution)/shard_map/project_q/pallas_call | solution.py:47
  404.4 0.0 all-gather.31.cloned.1.call-done
  404.4 0.0 all-gather.29.cloned.1.call-done
  404.4 88.1 %attention.4 = bf16[4,256,4096]{2,1,0:T(8,128)(2,1)} custom-call(s32[1]{0:T(128)} %bitcast.me_ref, bf16[16,256,4096]{2,1,0:T(8,128)(2,1)} %bitcast.59, bf16[8,4,256,1024]{3,2,1,0:T(8,128)(2,1)} %bitcast.52, bf16[8,4,1024,256]{3,2,1,0:T(8,128)(2,1)} %bitcast.51), custom_call_target="tpu_custom_call" | custom-call | flops 34359738368 | bytes 50331648 | tf_op jit(solution)/shard_map/attention/pallas_call | solution.py:164
  492.5 52.7 %project_o.4.rest_0_ = bf16[4096,5120]{1,0:T(8,128)(2,1)} custom-call(bf16[1024,4096]{1,0:T(8,128)(2,1)} %bitcast.63, bf16[4096,5120]{1,0:T(8,128)(2,1)} %bitcast.39, bf16[4096,5120]{1,0:T(8,128)(2,1)} %bitcast.35), custom_call_target="tpu_custom_call" | custom-call | flops 42949672960 | bytes 71303168 | tf_op jit(solution)/shard_map/project_o/pallas_call | solution.py:214
  545.2 0.0 all-gather.25.cloned.1.call-done
  545.3 0.0 all-gather.27.cloned.1.call-done
  545.3 88.7 %attention.5 = bf16[4,256,4096]{2,1,0:T(8,128)(2,1)} custom-call(s32[1]{0:T(128)} %bitcast.me_ref, bf16[16,256,4096]{2,1,0:T(8,128)(2,1)} %bitcast.60, bf16[8,4,256,1024]{3,2,1,0:T(8,128)(2,1)} %bitcast.53, bf16[8,4,1024,256]{3,2,1,0:T(8,128)(2,1)} %bitcast.54, bf16[4096,5120]{1,0:T(8,128)(2,1)} %project_o.4.rest_0_), custom_call_target="tpu_custom_call" | custom-call | flops 34359738368 | bytes 50331648 | tf_op jit(solution)/shard_map/attention/pallas_call | solution.py:164
  633.9 52.7 %project_o.5.rest_0_ = bf16[4096,5120]{1,0:T(8,128)(2,1)} custom-call(bf16[1024,4096]{1,0:T(8,128)(2,1)} %bitcast.48, bf16[4096,5120]{1,0:T(8,128)(2,1)} %bitcast.40, bf16[4096,5120]{1,0:T(8,128)(2,1)} %bitcast.36, bf16[4096,5120]{1,0:T(8,128)(2,1)} %project_o.4.rest_0_), custom_call_target="tpu_custom_call", output_to_operand_aliasing={{}: (3, {})} | custom-call | flops 42949672960 | bytes 71303168 | tf_op jit(solution)/shard_map/project_o/pallas_call | solution.py:214
  686.7 0.0 all-gather.21.cloned.1.call-done
  686.7 0.0 all-gather.23.cloned.1.call-done
  686.7 88.7 %attention.6 = bf16[4,256,4096]{2,1,0:T(8,128)(2,1)} custom-call(s32[1]{0:T(128)} %bitcast.me_ref, bf16[16,256,4096]{2,1,0:T(8,128)(2,1)} %bitcast.61, bf16[8,4,256,1024]{3,2,1,0:T(8,128)(2,1)} %bitcast.55, bf16[8,4,1024,256]{3,2,1,0:T(8,128)(2,1)} %bitcast.56, bf16[4096,5120]{1,0:T(8,128)(2,1)} %project_o.5.rest_0_), custom_call_target="tpu_custom_call" | custom-call | flops 34359738368 | bytes 50331648 | tf_op jit(solution)/shard_map/attention/pallas_call | solution.py:164
  775.4 52.7 %project_o.6.rest_0_ = bf16[4096,5120]{1,0:T(8,128)(2,1)} custom-call(bf16[1024,4096]{1,0:T(8,128)(2,1)} %bitcast.49, bf16[4096,5120]{1,0:T(8,128)(2,1)} %bitcast.41, bf16[4096,5120]{1,0:T(8,128)(2,1)} %bitcast.37, bf16[4096,5120]{1,0:T(8,128)(2,1)} %project_o.5.rest_0_), custom_call_target="tpu_custom_call", output_to_operand_aliasing={{}: (3, {})} | custom-call | flops 42949672960 | bytes 71303168 | tf_op jit(solution)/shard_map/project_o/pallas_call | solution.py:214
  828.2 0.0 all-gather.17.cloned.1.call-done
  828.2 0.0 all-gather.19.cloned.1.call-done
  828.2 88.8 %attention.7 = bf16[4,256,4096]{2,1,0:T(8,128)(2,1)} custom-call(s32[1]{0:T(128)} %bitcast.me_ref, bf16[16,256,4096]{2,1,0:T(8,128)(2,1)} %bitcast.62, bf16[8,4,256,1024]{3,2,1,0:T(8,128)(2,1)} %bitcast.57, bf16[8,4,1024,256]{3,2,1,0:T(8,128)(2,1)} %bitcast.58, bf16[4096,5120]{1,0:T(8,128)(2,1)} %project_o.6.rest_0_), custom_call_target="tpu_custom_call" | custom-call | flops 34359738368 | bytes 50331648 | tf_op jit(solution)/shard_map/attention/pallas_call | solution.py:164
  916.9 52.7 %project_o.7 = bf16[4096,5120]{1,0:T(8,128)(2,1)} custom-call(bf16[1024,4096]{1,0:T(8,128)(2,1)} %bitcast.47, bf16[4096,5120]{1,0:T(8,128)(2,1)} %bitcast.42, bf16[4096,5120]{1,0:T(8,128)(2,1)} %bitcast.38, bf16[4096,5120]{1,0:T(8,128)(2,1)} %project_o.6.rest_0_), custom_call_target="tpu_custom_call", output_to_operand_aliasing={{}: (3, {})} | custom-call | flops 42949672960 | bytes 71303168 | tf_op jit(solution)/shard_map/project_o/pallas_call | solution.py:214
  (2 shorter events, 0.0 us)
Async XLA Ops:
  6.5 397.9 %all-gather.31.cloned.1.call-start = ((), (), s32[]{:S(2)}) async-start(), calls=%async_computation.7 | async-start | bytes 18874368 | tf_op jit(solution)/shard_map/all_gather | solution.py:241
  72.0 332.4 %all-gather.29.cloned.1.call-start = ((), (), s32[]{:S(2)}) async-start(), calls=%async_computation.6 | async-start | bytes 18874368 | tf_op jit(solution)/shard_map/all_gather | solution.py:241
  72.8 472.5 %all-gather.25.cloned.1.call-start = ((), (), s32[]{:S(2)}) async-start(), calls=%async_computation.4 | async-start | bytes 18874368 | tf_op jit(solution)/shard_map/all_gather | solution.py:241
  106.0 439.2 %all-gather.27.cloned.1.call-start = ((), (), s32[]{:S(2)}) async-start(), calls=%async_computation.5 | async-start | bytes 18874368 | tf_op jit(solution)/shard_map/all_gather | solution.py:241
  106.6 580.0 %all-gather.21.cloned.1.call-start = ((), (), s32[]{:S(2)}) async-start(), calls=%async_computation.2 | async-start | bytes 18874368 | tf_op jit(solution)/shard_map/all_gather | solution.py:241
  140.0 546.7 %all-gather.23.cloned.1.call-start = ((), (), s32[]{:S(2)}) async-start(), calls=%async_computation.3 | async-start | bytes 18874368 | tf_op jit(solution)/shard_map/all_gather | solution.py:241
  140.6 687.6 %all-gather.17.cloned.1.call-start = ((), (), s32[]{:S(2)}) async-start(), calls=%async_computation | async-start | bytes 18874368 | tf_op jit(solution)/shard_map/all_gather | solution.py:241
  174.0 654.1 %all-gather.19.cloned.1.call-start = ((), (), s32[]{:S(2)}) async-start(), calls=%async_computation.1 | async-start | bytes 18874368 | tf_op jit(solution)/shard_map/all_gather | solution.py:241
Sparse Core Ops, SparseCore 0:
  72.2 84.0 all-gather.30
  158.1 84.0 all-gather.28
  244.0 84.0 all-gather.24
  329.8 84.0 all-gather.26
  415.6 84.1 all-gather.20
  501.4 84.0 all-gather.22
  587.3 84.0 all-gather.16
  673.3 84.0 all-gather.18

commit v2 on v1

--- a/solution.py
+++ b/solution.py
@@ -35,26 +35,26 @@
         at = pl.ds(pl.multiple_of(r * step, step), step)
         x = x_ref[at, :]
         cos, sin = cos_ref[at, :], sin_ref[at, :]
-        for c in range(0, width, 256):
-            acc = jnp.dot(x, w_ref[:, c:c + 256], preferred_element_type=jnp.float32)
-            o_ref[at, c:c + HEAD] = rope_round(acc[:, :HEAD], cos, sin)
-            o_ref[at, c + HEAD:c + 256] = rope_round(acc[:, HEAD:], cos, sin)
-
-
-def project_q(x, w, cos, sin, tile_m=1024, tile_n=512):
+        for c in range(0, width, 512):
+            acc = jnp.dot(x, w_ref[:, c:c + 512], preferred_element_type=jnp.float32)
+            for h in range(0, 512, HEAD):
+                o_ref[at, c + h:c + h + HEAD] = rope_round(acc[:, h:h + HEAD], cos, sin)
+
+
+def project_q(x, w, cos, sin, tile_m=512, tile_n=1024):
     m, d = x.shape
     n = w.shape[1]
     return pl.pallas_call(
         q_kernel,
         out_shape=jax.ShapeDtypeStruct((m, n), jnp.bfloat16),
-        grid=(m // tile_m, n // tile_n),
+        grid=(n // tile_n, m // tile_m),
         in_specs=[
-            pl.BlockSpec((tile_m, d), lambda i, j: (i, 0)),
-            pl.BlockSpec((d, tile_n), lambda i, j: (0, j)),
-            pl.BlockSpec((tile_m, HEAD), lambda i, j: (i, 0)),
-            pl.BlockSpec((tile_m, HEAD), lambda i, j: (i, 0)),
+            pl.BlockSpec((tile_m, d), lambda j, i: (i, 0)),
+            pl.BlockSpec((d, tile_n), lambda j, i: (0, j)),
+            pl.BlockSpec((tile_m, HEAD), lambda j, i: (i, 0)),
+            pl.BlockSpec((tile_m, HEAD), lambda j, i: (i, 0)),
         ],
-        out_specs=pl.BlockSpec((tile_m, tile_n), lambda i, j: (i, j)),
+        out_specs=pl.BlockSpec((tile_m, tile_n), lambda j, i: (i, j)),
         compiler_params=pltpu.CompilerParams(vmem_limit_bytes=VMEM_LIMIT),
         cost_estimate=pl.CostEstimate(flops=2 * m * n * d, bytes_accessed=2 * (m * d + m * n + 4 * n * d), transcendentals=0),
         name="project_q",
@@ -64,17 +64,15 @@
 def kv_kernel(x_ref, wk_ref, wv_ref, cos_ref, sin_ref, k_ref, v_ref):
     seqs, tok = v_ref.shape[0], v_ref.shape[2]
 
-    @pl.loop(0, seqs)
-    def _(s):
-        at = pl.ds(pl.multiple_of(s * tok, tok), tok)
-        x = x_ref[at, :]
-        cos, sin = cos_ref[at, :], sin_ref[at, :]
-        for c in range(0, wk_ref.shape[1], 256):
-            acc = jnp.dot(x, wk_ref[:, c:c + 256], preferred_element_type=jnp.float32)
-            k_ref[s, :, c:c + HEAD] = rope_round(acc[:, :HEAD], cos, sin)
-            k_ref[s, :, c + HEAD:c + 256] = rope_round(acc[:, HEAD:], cos, sin)
-            acc = jnp.dot(x, wv_ref[:, c:c + 256], preferred_element_type=jnp.float32)
-            v_ref[s, c:c + 256, :] = acc.T.astype(jnp.bfloat16)
+    x = x_ref[...]
+    cos, sin = cos_ref[...], sin_ref[...]
+    for c in range(0, wk_ref.shape[1], 256):
+        acc = jnp.dot(x, wk_ref[:, c:c + 256], preferred_element_type=jnp.float32)
+        for h in range(0, 256, HEAD):
+            k_ref[:, :, c + h:c + h + HEAD] = rope_round(acc[:, h:h + HEAD], cos, sin).reshape(seqs, tok, HEAD)
+        acc = jnp.dot(x, wv_ref[:, c:c + 256], preferred_element_type=jnp.float32)
+        for s in range(seqs):
+            v_ref[s, c:c + 256, :] = acc[s * tok:(s + 1) * tok, :].T.astype(jnp.bfloat16)
 
 
 def project_kv(x, w_k, w_v, cos, sin, seq0, seqs, tok, tile_n=256):
@@ -111,6 +109,7 @@
     me = me_ref[0]
     tok = q_ref.shape[1]
     heads = q_ref.shape[2] // HEAD
+    per_kv = heads // (k_ref.shape[3] // HEAD)
     scale = HEAD ** -0.5 * LOG2E
     bufs = (s_even, s_odd)
 
@@ -118,8 +117,9 @@
         buf = bufs[h % 2]
         q = q_ref[0, :, h * HEAD:(h + 1) * HEAD]
         top = jnp.full((8, tok), -jnp.inf, jnp.float32)
+        kv = slice(h // per_kv * HEAD, (h // per_kv + 1) * HEAD)
         for j in range(blocks):
-            s = lax.dot_general(k_ref[j, 0], q, (((1,), (1,)), ((), ())), preferred_element_type=jnp.float32)
+            s = lax.dot_general(k_ref[j, 0, :, kv], q, (((1,), (1,)), ((), ())), preferred_element_type=jnp.float32)
             if j >= first_masked:
                 key = lax.broadcasted_iota(jnp.int32, (tok, tok), 0) + j * tok
                 row = lax.broadcasted_iota(jnp.int32, (tok, tok), 1) + me * tok
@@ -133,10 +133,11 @@
         shift = top * scale
         total = jnp.zeros((8, tok), jnp.float32)
         acc = None
+        kv = slice(h // per_kv * HEAD, (h // per_kv + 1) * HEAD)
         for j in range(blocks):
             p = jnp.exp2(buf[j * tok:(j + 1) * tok, :] * scale - shift)
             total = total + jnp.sum(p.reshape(tok // 8, 8, tok), axis=0)
-            part = jnp.dot(v_ref[j, 0], p.astype(jnp.bfloat16), preferred_element_type=jnp.float32)
+            part = jnp.dot(v_ref[j, 0, kv, :], p.astype(jnp.bfloat16), preferred_element_type=jnp.float32)
             acc = part if acc is None else acc + part
         out = acc * (1.0 / jnp.sum(total, axis=0, keepdims=True))
         o_ref[0, :, h * HEAD:(h + 1) * HEAD] = out.T.astype(jnp.bfloat16)
@@ -156,21 +157,21 @@
             run(2 * pair + 2, 2 * pair)
 
 
-def attention(me, q, k_all, v_all, seq0, after):
+def attention(me, q, k_all, v_all, seq0, after, kv_heads=2):
     n_dev, seqs, tok, kv_width = k_all.shape
     n_kv = kv_width // HEAD
-    width = q.shape[2] // n_kv
+    width = q.shape[2] // n_kv * kv_heads
     flops = 4 * seqs * tok * n_dev * tok * q.shape[2]
     return pl.pallas_call(
         attn_kernel,
         out_shape=jax.ShapeDtypeStruct((seqs, tok, q.shape[2]), jnp.bfloat16),
         grid_spec=pltpu.PrefetchScalarGridSpec(
             num_scalar_prefetch=1,
-            grid=(seqs, n_kv),
+            grid=(seqs, n_kv // kv_heads),
             in_specs=[
                 pl.BlockSpec((1, tok, width), lambda b, g, me: (b + seq0 if seq0 else b, 0, g)),
-                pl.BlockSpec((n_dev, 1, tok, HEAD), lambda b, g, me: (0, b, 0, g)),
-                pl.BlockSpec((n_dev, 1, HEAD, tok), lambda b, g, me: (0, b, g, 0)),
+                pl.BlockSpec((n_dev, 1, tok, kv_heads * HEAD), lambda b, g, me: (0, b, 0, g)),
+                pl.BlockSpec((n_dev, 1, kv_heads * HEAD, tok), lambda b, g, me: (0, b, g, 0)),
             ] + [pl.BlockSpec(memory_space=pl.ANY)] * len(after),
             out_specs=pl.BlockSpec((1, tok, width), lambda b, g, me: (b, 0, g)),
             scratch_shapes=[pltpu.VMEM((n_dev * tok, tok), jnp.float32)] * 2,
@@ -183,16 +184,10 @@
 
 def o_kernel(o_ref, w_ref, x_ref, *rest):
     y_ref = rest[-1]
-    rows = o_ref.shape[0]
-    step = 512
-
-    @pl.loop(0, rows // step)
-    def _(r):
-        at = pl.ds(pl.multiple_of(r * step, step), step)
-        a = o_ref[at, :]
-        for c in range(0, w_ref.shape[1], 256):
-            acc = jnp.dot(a, w_ref[:, c:c + 256], preferred_element_type=jnp.float32)
-            y_ref[at, c:c + 256] = (x_ref[at, c:c + 256].astype(jnp.float32) + acc).astype(jnp.bfloat16)
+    a = o_ref[...]
+    for c in range(0, w_ref.shape[1], 256):
+        acc = jnp.dot(a, w_ref[:, c:c + 256], preferred_element_type=jnp.float32)
+        y_ref[:, c:c + 256] = (x_ref[:, c:c + 256].astype(jnp.float32) + acc).astype(jnp.bfloat16)
 
 
 def project_o(o, w, x, y, row0, tile_n=512):
@@ -230,7 +225,7 @@
         x = hidden.reshape(seqs * tok, d)
         w_q = w_q.reshape(d, -1)
         w_k = w_k.reshape(d, -1)
-        w_v = w_v.reshape(d, -1)
+        w_v = lax.optimization_barrier((w_v, w_k))[0].reshape(d, -1)
         w_o = w_o.reshape(-1, d)
         cos, sin = rope_tables(positions)
         me = lax.axis_index('cp').astype(jnp.int32).reshape(1)

time: 989 us -> 932 us (0.942)
  Pallas kernels: 899 us -> 849 us
    pallas_call x4, Pallas kernels: 354 us -> 330 us  [attention(): pl.pallas_call(attn_kernel, out_shape=jax.ShapeDtypeStruct((seqs, tok, q....]
    unnamed x2 -> x4, local copies, waits for them, and re-layouts: 28.7 us -> 50.1 us
    reshape x1 -> x0, local copies, waits for them, and re-layouts: 20.9 us -> none  [per_device(): w_v = w_v.reshape(d, -1)]
    pallas_call x4, Pallas kernels: 133 us -> 121 us  [project_kv(): pl.pallas_call(kv_kernel, out_shape=(jax.ShapeDtypeStruct((seqs, tok, n),...]
where the time goes in v2:
time: 932 us; the launch traced here: 927 us
  Pallas kernels  849 us (91%)
  local copies, waits for them, and re-layouts  50.1 us (5%)
  between operations  13.9 us (1%)
  other arithmetic  11.6 us (1%)
    pallas_call x4, Pallas kernels, attention(): pl.pallas_call(attn_kernel, out_shape=jax.ShapeDtypeStruct((seqs, tok, q....  330 us
    pallas_call x4, Pallas kernels, project_o(): pl.pallas_call(o_kernel, out_shape=jax.ShapeDtypeStruct((m, d), jnp.bfloa...  204 us
    pallas_call x1, Pallas kernels, project_q(): pl.pallas_call(q_kernel, out_shape=jax.ShapeDtypeStruct((m, n), jnp.bfloa...  194 us
    pallas_call x4, Pallas kernels, project_kv(): pl.pallas_call(kv_kernel, out_shape=(jax.ShapeDtypeStruct((seqs, tok, n),...  121 us
    unnamed x4, local copies, waits for them, and re-layouts  50.1 us
  transfers between devices with their start and end apart: 8, of which 0 were waited for; matrix products, arithmetic and copies ran while one was open for 3% of the time, Pallas kernels for 74%

profile of v2, /device:TPU:6, one launch (start us, length us, event | category | flops | bytes accessed | tf_op | source)
XLA Modules:
  0.0 927.0 jit_solution(15980865515814164881)
XLA Ops:
  6.5 0.0 all-gather.31.cloned.1.call-start
  6.5 0.7 convert_bitcast_fusion
  7.3 10.8 %copy.19 = bf16[640,8,8,128]{3,1,2,0:T(8,128)(2,1)} copy(bf16[640,8,8,128]{3,2,1,0:T(8,128)(2,1)} %bitcast.47) | data formatting | bytes 20971520
  18.1 10.7 %copy.18 = bf16[640,8,8,128]{3,1,2,0:T(8,128)(2,1)} copy(bf16[640,8,8,128]{3,2,1,0:T(8,128)(2,1)} %bitcast.48) | data formatting | bytes 20971520
  28.8 7.7 fusion
  36.4 3.2 pad_maximum_fusion
  39.6 30.0 %project_kv.7 = (bf16[4,256,1024]{2,1,0:T(8,128)(2,1)}, bf16[4,1024,256]{2,1,0:T(8,128)(2,1)}) custom-call(bf16[4096,5120]{1,0:T(8,128)(2,1)} %bitcast.32, bf16[5120,1024]{1,0:T(8,128)(2,1)} %bitcast.49, bf16[5120,1024]{1,0:T(8,128)(2,1)} %bitcast.53, f32[4096,128]{1,0:T(8,128)} %get-tuple-element.26.cos_ref, f32[4096,128]{1,0:T(8,128)} %get-tuple-element.27.sin_ref), custom_call_target="tpu_custom_call" | custom-call | flops 21474836480 | bytes 35651584 | tf_op jit(solution)/shard_map/project_kv/pallas_call | solution.py:83
  69.6 0.0 all-gather.31.cloned.1.call-update
  69.6 0.0 all-gather.29.cloned.1.call-start
  69.7 0.7 all-gather.29.cloned.1.call-update
  70.4 0.0 all-gather.25.cloned.1.call-start
  70.4 30.5 %project_kv.6 = (bf16[4,256,1024]{2,1,0:T(8,128)(2,1)}, bf16[4,1024,256]{2,1,0:T(8,128)(2,1)}) custom-call(bf16[4096,5120]{1,0:T(8,128)(2,1)} %bitcast.33, bf16[5120,1024]{1,0:T(8,128)(2,1)} %bitcast.50, bf16[5120,1024]{1,0:T(8,128)(2,1)} %bitcast.54, f32[4096,128]{1,0:T(8,128)} %get-tuple-element.26.cos_ref, f32[4096,128]{1,0:T(8,128)} %get-tuple-element.27.sin_ref), custom_call_target="tpu_custom_call" | custom-call | flops 21474836480 | bytes 35651584 | tf_op jit(solution)/shard_map/project_kv/pallas_call | solution.py:83
  100.9 0.0 all-gather.25.cloned.1.call-update
  100.9 0.0 all-gather.27.cloned.1.call-start
  101.0 0.5 all-gather.27.cloned.1.call-update
  101.5 0.0 all-gather.21.cloned.1.call-start
  101.6 30.1 %project_kv.5 = (bf16[4,256,1024]{2,1,0:T(8,128)(2,1)}, bf16[4,1024,256]{2,1,0:T(8,128)(2,1)}) custom-call(bf16[4096,5120]{1,0:T(8,128)(2,1)} %bitcast.34, bf16[5120,1024]{1,0:T(8,128)(2,1)} %bitcast.51, bf16[5120,1024]{1,0:T(8,128)(2,1)} %bitcast.55, f32[4096,128]{1,0:T(8,128)} %get-tuple-element.26.cos_ref, f32[4096,128]{1,0:T(8,128)} %get-tuple-element.27.sin_ref), custom_call_target="tpu_custom_call" | custom-call | flops 21474836480 | bytes 35651584 | tf_op jit(solution)/shard_map/project_kv/pallas_call | solution.py:83
  131.6 0.0 all-gather.21.cloned.1.call-update
  131.7 0.0 all-gather.23.cloned.1.call-start
  131.7 0.5 all-gather.23.cloned.1.call-update
  132.3 0.0 all-gather.17.cloned.1.call-start
  132.3 30.1 %project_kv.4 = (bf16[4,256,1024]{2,1,0:T(8,128)(2,1)}, bf16[4,1024,256]{2,1,0:T(8,128)(2,1)}) custom-call(bf16[4096,5120]{1,0:T(8,128)(2,1)} %bitcast.35, bf16[5120,1024]{1,0:T(8,128)(2,1)} %bitcast.52, bf16[5120,1024]{1,0:T(8,128)(2,1)} %bitcast.56, f32[4096,128]{1,0:T(8,128)} %get-tuple-element.26.cos_ref, f32[4096,128]{1,0:T(8,128)} %get-tuple-element.27.sin_ref), custom_call_target="tpu_custom_call" | custom-call | flops 21474836480 | bytes 35651584 | tf_op jit(solution)/shard_map/project_kv/pallas_call | solution.py:83
  162.4 0.0 all-gather.17.cloned.1.call-update
  162.4 0.0 all-gather.19.cloned.1.call-start
  162.4 0.7 all-gather.19.cloned.1.call-update
  163.1 28.6 %copy.17 = bf16[640,8,32,128]{3,1,2,0:T(8,128)(2,1)} copy(bf16[640,8,32,128]{3,2,1,0:T(8,128)(2,1)} %bitcast.45) | data formatting | bytes 83886080
  191.8 193.9 %project_q.1 = bf16[4096,4096]{1,0:T(8,128)(2,1)} custom-call(bf16[4096,5120]{1,0:T(8,128)(2,1)} %bitcast.36, bf16[5120,4096]{1,0:T(8,128)(2,1)} %bitcast.46, f32[4096,128]{1,0:T(8,128)} %get-tuple-element.26.cos_ref, f32[4096,128]{1,0:T(8,128)} %get-tuple-element.27.sin_ref), custom_call_target="tpu_custom_call" | custom-call | flops 171798691840 | bytes 243269632 | tf_op jit(solution)/shard_map/project_q/pallas_call | solution.py:47
  385.6 0.0 all-gather.31.cloned.1.call-done
  385.6 0.0 all-gather.29.cloned.1.call-done
  385.6 82.4 %attention.4 = bf16[4,256,4096]{2,1,0:T(8,128)(2,1)} custom-call(s32[1]{0:T(128)} %bitcast.me_ref, bf16[16,256,4096]{2,1,0:T(8,128)(2,1)} %bitcast.69, bf16[8,4,256,1024]{3,2,1,0:T(8,128)(2,1)} %bitcast.62, bf16[8,4,1024,256]{3,2,1,0:T(8,128)(2,1)} %bitcast.61), custom_call_target="tpu_custom_call" | custom-call | flops 34359738368 | bytes 50331648 | tf_op jit(solution)/shard_map/attention/pallas_call | solution.py:165
  468.0 51.0 %project_o.4.rest_0_ = bf16[4096,5120]{1,0:T(8,128)(2,1)} custom-call(bf16[1024,4096]{1,0:T(8,128)(2,1)} %bitcast.73, bf16[4096,5120]{1,0:T(8,128)(2,1)} %bitcast.41, bf16[4096,5120]{1,0:T(8,128)(2,1)} %bitcast.37), custom_call_target="tpu_custom_call" | custom-call | flops 42949672960 | bytes 71303168 | tf_op jit(solution)/shard_map/project_o/pallas_call | solution.py:209
  519.0 0.0 all-gather.25.cloned.1.call-done
  519.0 0.0 all-gather.27.cloned.1.call-done
  519.0 82.7 %attention.5 = bf16[4,256,4096]{2,1,0:T(8,128)(2,1)} custom-call(s32[1]{0:T(128)} %bitcast.me_ref, bf16[16,256,4096]{2,1,0:T(8,128)(2,1)} %bitcast.70, bf16[8,4,256,1024]{3,2,1,0:T(8,128)(2,1)} %bitcast.63, bf16[8,4,1024,256]{3,2,1,0:T(8,128)(2,1)} %bitcast.64, bf16[4096,5120]{1,0:T(8,128)(2,1)} %project_o.4.rest_0_), custom_call_target="tpu_custom_call" | custom-call | flops 34359738368 | bytes 50331648 | tf_op jit(solution)/shard_map/attention/pallas_call | solution.py:165
  601.8 51.0 %project_o.5.rest_0_ = bf16[4096,5120]{1,0:T(8,128)(2,1)} custom-call(bf16[1024,4096]{1,0:T(8,128)(2,1)} %bitcast.58, bf16[4096,5120]{1,0:T(8,128)(2,1)} %bitcast.42, bf16[4096,5120]{1,0:T(8,128)(2,1)} %bitcast.38, bf16[4096,5120]{1,0:T(8,128)(2,1)} %project_o.4.rest_0_), custom_call_target="tpu_custom_call", output_to_operand_aliasing={{}: (3, {})} | custom-call | flops 42949672960 | bytes 71303168 | tf_op jit(solution)/shard_map/project_o/pallas_call | solution.py:209
  652.8 0.0 all-gather.21.cloned.1.call-done
  652.8 0.0 all-gather.23.cloned.1.call-done
  652.8 82.5 %attention.6 = bf16[4,256,4096]{2,1,0:T(8,128)(2,1)} custom-call(s32[1]{0:T(128)} %bitcast.me_ref, bf16[16,256,4096]{2,1,0:T(8,128)(2,1)} %bitcast.71, bf16[8,4,256,1024]{3,2,1,0:T(8,128)(2,1)} %bitcast.65, bf16[8,4,1024,256]{3,2,1,0:T(8,128)(2,1)} %bitcast.66, bf16[4096,5120]{1,0:T(8,128)(2,1)} %project_o.5.rest_0_), custom_call_target="tpu_custom_call" | custom-call | flops 34359738368 | bytes 50331648 | tf_op jit(solution)/shard_map/attention/pallas_call | solution.py:165
  735.2 51.0 %project_o.6.rest_0_ = bf16[4096,5120]{1,0:T(8,128)(2,1)} custom-call(bf16[1024,4096]{1,0:T(8,128)(2,1)} %bitcast.59, bf16[4096,5120]{1,0:T(8,128)(2,1)} %bitcast.43, bf16[4096,5120]{1,0:T(8,128)(2,1)} %bitcast.39, bf16[4096,5120]{1,0:T(8,128)(2,1)} %project_o.5.rest_0_), custom_call_target="tpu_custom_call", output_to_operand_aliasing={{}: (3, {})} | custom-call | flops 42949672960 | bytes 71303168 | tf_op jit(solution)/shard_map/project_o/pallas_call | solution.py:209
  786.2 0.0 all-gather.17.cloned.1.call-done
  786.2 0.0 all-gather.19.cloned.1.call-done
  786.2 82.5 %attention.7 = bf16[4,256,4096]{2,1,0:T(8,128)(2,1)} custom-call(s32[1]{0:T(128)} %bitcast.me_ref, bf16[16,256,4096]{2,1,0:T(8,128)(2,1)} %bitcast.72, bf16[8,4,256,1024]{3,2,1,0:T(8,128)(2,1)} %bitcast.67, bf16[8,4,1024,256]{3,2,1,0:T(8,128)(2,1)} %bitcast.68, bf16[4096,5120]{1,0:T(8,128)(2,1)} %project_o.6.rest_0_), custom_call_target="tpu_custom_call" | custom-call | flops 34359738368 | bytes 50331648 | tf_op jit(solution)/shard_map/attention/pallas_call | solution.py:165
  868.8 51.0 %project_o.7 = bf16[4096,5120]{1,0:T(8,128)(2,1)} custom-call(bf16[1024,4096]{1,0:T(8,128)(2,1)} %bitcast.57, bf16[4096,5120]{1,0:T(8,128)(2,1)} %bitcast.44, bf16[4096,5120]{1,0:T(8,128)(2,1)} %bitcast.40, bf16[4096,5120]{1,0:T(8,128)(2,1)} %project_o.6.rest_0_), custom_call_target="tpu_custom_call", output_to_operand_aliasing={{}: (3, {})} | custom-call | flops 42949672960 | bytes 71303168 | tf_op jit(solution)/shard_map/project_o/pallas_call | solution.py:209
  (2 shorter events, 0.0 us)
Async XLA Ops:
  6.5 379.1 %all-gather.31.cloned.1.call-start = ((), (), s32[]{:S(2)}) async-start(), calls=%async_computation.7 | async-start | bytes 18874368 | tf_op jit(solution)/shard_map/all_gather | solution.py:236
  69.6 316.0 %all-gather.29.cloned.1.call-start = ((), (), s32[]{:S(2)}) async-start(), calls=%async_computation.6 | async-start | bytes 18874368 | tf_op jit(solution)/shard_map/all_gather | solution.py:236
  70.4 448.6 %all-gather.25.cloned.1.call-start = ((), (), s32[]{:S(2)}) async-start(), calls=%async_computation.4 | async-start | bytes 18874368 | tf_op jit(solution)/shard_map/all_gather | solution.py:236
  100.9 418.1 %all-gather.27.cloned.1.call-start = ((), (), s32[]{:S(2)}) async-start(), calls=%async_computation.5 | async-start | bytes 18874368 | tf_op jit(solution)/shard_map/all_gather | solution.py:236
  101.5 551.2 %all-gather.21.cloned.1.call-start = ((), (), s32[]{:S(2)}) async-start(), calls=%async_computation.2 | async-start | bytes 18874368 | tf_op jit(solution)/shard_map/all_gather | solution.py:236
  131.7 521.1 %all-gather.23.cloned.1.call-start = ((), (), s32[]{:S(2)}) async-start(), calls=%async_computation.3 | async-start | bytes 18874368 | tf_op jit(solution)/shard_map/all_gather | solution.py:236
  132.3 654.0 %all-gather.17.cloned.1.call-start = ((), (), s32[]{:S(2)}) async-start(), calls=%async_computation | async-start | bytes 18874368 | tf_op jit(solution)/shard_map/all_gather | solution.py:236
  162.4 623.9 %all-gather.19.cloned.1.call-start = ((), (), s32[]{:S(2)}) async-start(), calls=%async_computation.1 | async-start | bytes 18874368 | tf_op jit(solution)/shard_map/all_gather | solution.py:236
Sparse Core Ops, SparseCore 0:
  69.8 84.0 all-gather.30
  155.7 84.0 all-gather.28
  241.6 84.0 all-gather.24
  327.4 84.0 all-gather.26
  413.2 84.0 all-gather.20
  499.0 84.0 all-gather.22
  584.9 84.0 all-gather.16
  670.8 84.0 all-gather.18

commit v3 on v2

--- a/solution.py
+++ b/solution.py
@@ -11,7 +11,7 @@
 HEAD = 128
 LOG2E = 1.4426950408889634
 VMEM_LIMIT = 60 * 1024 * 1024
-CHUNKS = (4, 4, 4, 4)
+CHUNKS = 4
 
 
 def rope_tables(positions):
@@ -61,47 +61,62 @@
     )(x, w, cos, sin)
 
 
-def kv_kernel(x_ref, wk_ref, wv_ref, cos_ref, sin_ref, k_ref, v_ref):
-    seqs, tok = v_ref.shape[0], v_ref.shape[2]
-
-    x = x_ref[...]
-    cos, sin = cos_ref[...], sin_ref[...]
-    for c in range(0, wk_ref.shape[1], 256):
-        acc = jnp.dot(x, wk_ref[:, c:c + 256], preferred_element_type=jnp.float32)
-        for h in range(0, 256, HEAD):
-            k_ref[:, :, c + h:c + h + HEAD] = rope_round(acc[:, h:h + HEAD], cos, sin).reshape(seqs, tok, HEAD)
-        acc = jnp.dot(x, wv_ref[:, c:c + 256], preferred_element_type=jnp.float32)
-        for s in range(seqs):
-            v_ref[s, c:c + 256, :] = acc[s * tok:(s + 1) * tok, :].T.astype(jnp.bfloat16)
-
-
-def project_kv(x, w_k, w_v, cos, sin, seq0, seqs, tok, tile_n=256):
+def kv_kernel(x_ref, wk_ref, wv_ref, cos_ref, sin_ref, *out_refs):
+    seqs, tok = out_refs[1].shape[0], out_refs[1].shape[2]
+
+    def run(k_ref, v_ref):
+        x = x_ref[...]
+        cos, sin = cos_ref[...], sin_ref[...]
+        for c in range(0, wk_ref.shape[1], 256):
+            acc = jnp.dot(x, wk_ref[:, c:c + 256], preferred_element_type=jnp.float32)
+            for h in range(0, 256, HEAD):
+                k_ref[:, :, c + h:c + h + HEAD] = rope_round(acc[:, h:h + HEAD], cos, sin).reshape(seqs, tok, HEAD)
+            acc = jnp.dot(x, wv_ref[:, c:c + 256], preferred_element_type=jnp.float32)
+            for s in range(seqs):
+                v_ref[s, c:c + 256, :] = acc[s * tok:(s + 1) * tok, :].T.astype(jnp.bfloat16)
+
+    if len(out_refs) == 2:
+        run(*out_refs)
+    else:
+        for c in range(len(out_refs) // 2):
+            pl.when(pl.program_id(0) == c)(functools.partial(run, *out_refs[2 * c:2 * c + 2]))
+
+
+def project_kv(x, w_k, w_v, cos, sin, chunk0, chunks, seqs, tok, tile_n=256):
     d, n = w_k.shape
     rows = seqs * tok
-    assert seq0 % seqs == 0
-    i0 = seq0 // seqs
-    return pl.pallas_call(
+    tiles = n // tile_n
+
+    def tile_of(chunk):
+        return lambda i, j: jnp.where(i < chunk, 0, jnp.where(i == chunk, j, tiles - 1))
+
+    def specs_of(chunk):
+        at = tile_of(chunk)
+        return [
+            pl.BlockSpec((seqs, tok, tile_n), lambda i, j: (0, 0, at(i, j))),
+            pl.BlockSpec((seqs, tile_n, tok), lambda i, j: (0, at(i, j), 0)),
+        ]
+
+    outs = pl.pallas_call(
         kv_kernel,
-        out_shape=(
+        out_shape=[
             jax.ShapeDtypeStruct((seqs, tok, n), jnp.bfloat16),
             jax.ShapeDtypeStruct((seqs, n, tok), jnp.bfloat16),
-        ),
-        grid=(n // tile_n,),
+        ] * chunks,
+        grid=(chunks, tiles),
         in_specs=[
-            pl.BlockSpec((rows, d), lambda j: (i0, 0)),
-            pl.BlockSpec((d, tile_n), lambda j: (0, j)),
-            pl.BlockSpec((d, tile_n), lambda j: (0, j)),
-            pl.BlockSpec((rows, HEAD), lambda j: (i0, 0)),
-            pl.BlockSpec((rows, HEAD), lambda j: (i0, 0)),
+            pl.BlockSpec((rows, d), lambda i, j: (i + chunk0, 0)),
+            pl.BlockSpec((d, tile_n), lambda i, j: (0, j)),
+            pl.BlockSpec((d, tile_n), lambda i, j: (0, j)),
+            pl.BlockSpec((rows, HEAD), lambda i, j: (i + chunk0, 0)),
+            pl.BlockSpec((rows, HEAD), lambda i, j: (i + chunk0, 0)),
         ],
-        out_specs=(
-            pl.BlockSpec((seqs, tok, tile_n), lambda j: (0, 0, j)),
-            pl.BlockSpec((seqs, tile_n, tok), lambda j: (0, j, 0)),
-        ),
-        compiler_params=pltpu.CompilerParams(vmem_limit_bytes=VMEM_LIMIT),
-        cost_estimate=pl.CostEstimate(flops=4 * rows * n * d, bytes_accessed=2 * rows * d + 4 * n * d + 4 * rows * n, transcendentals=0),
+        out_specs=[spec for chunk in range(chunks) for spec in specs_of(chunk)],
+        compiler_params=pltpu.CompilerParams(vmem_limit_bytes=VMEM_LIMIT),
+        cost_estimate=pl.CostEstimate(flops=4 * chunks * rows * n * d, bytes_accessed=2 * chunks * rows * d + 4 * chunks * n * d + 4 * chunks * rows * n, transcendentals=0),
         name="project_kv",
     )(x, w_k, w_v, cos, sin)
+    return [(outs[2 * c], outs[2 * c + 1]) for c in range(chunks)]
 
 
 def attn_kernel(me_ref, q_ref, k_ref, v_ref, *rest):
@@ -119,7 +134,7 @@
         top = jnp.full((8, tok), -jnp.inf, jnp.float32)
         kv = slice(h // per_kv * HEAD, (h // per_kv + 1) * HEAD)
         for j in range(blocks):
-            s = lax.dot_general(k_ref[j, 0, :, kv], q, (((1,), (1,)), ((), ())), preferred_element_type=jnp.float32)
+            s = lax.dot_general(k_ref[j, 0, :, kv], q, (((1,), (1,)), ((), ())), preferred_element_type=jnp.float32) * scale
             if j >= first_masked:
                 key = lax.broadcasted_iota(jnp.int32, (tok, tok), 0) + j * tok
                 row = lax.broadcasted_iota(jnp.int32, (tok, tok), 1) + me * tok
@@ -130,12 +145,11 @@
 
     def apply(h, blocks, top):
         buf = bufs[h % 2]
-        shift = top * scale
         total = jnp.zeros((8, tok), jnp.float32)
         acc = None
         kv = slice(h // per_kv * HEAD, (h // per_kv + 1) * HEAD)
         for j in range(blocks):
-            p = jnp.exp2(buf[j * tok:(j + 1) * tok, :] * scale - shift)
+            p = jnp.exp2(buf[j * tok:(j + 1) * tok, :] - top)
             total = total + jnp.sum(p.reshape(tok // 8, 8, tok), axis=0)
             part = jnp.dot(v_ref[j, 0, kv, :], p.astype(jnp.bfloat16), preferred_element_type=jnp.float32)
             acc = part if acc is None else acc + part
@@ -151,10 +165,10 @@
                 apply(h - 1, blocks, tops[h - 1])
 
     n_dev = k_ref.shape[0]
-    for pair in range(n_dev // 2):
-        @pl.when(me // 2 == pair)
-        def _():
-            run(2 * pair + 2, 2 * pair)
+    low = 0
+    for high in [*range(n_dev - 6, n_dev - 1, 2), n_dev - 1]:
+        pl.when((me >= low) & (me <= high))(functools.partial(run, high + 1, low))
+        low = high + 1
 
 
 def attention(me, q, k_all, v_all, seq0, after, kv_heads=2):
@@ -229,19 +243,15 @@
         w_o = w_o.reshape(-1, d)
         cos, sin = rope_tables(positions)
         me = lax.axis_index('cp').astype(jnp.int32).reshape(1)
-        gathered = []
-        seq0 = 0
-        for n in CHUNKS:
-            k, v = project_kv(x, w_k, w_v, cos, sin, seq0, n, tok)
-            gathered.append((lax.all_gather(k, 'cp', axis=0), lax.all_gather(v, 'cp', axis=0)))
-            seq0 += n
+        n = seqs // CHUNKS
+        pairs = project_kv(x, w_k, w_v, cos, sin, 0, 1, n, tok)
+        pairs += project_kv(x, w_k, w_v, cos, sin, 1, CHUNKS - 1, n, tok)
+        gathered = [(lax.all_gather(k, 'cp', axis=0), lax.all_gather(v, 'cp', axis=0)) for k, v in pairs]
         q = project_q(x, w_q, cos, sin).reshape(seqs, tok, -1)
         y = None
-        seq0 = 0
-        for n, (k_all, v_all) in zip(CHUNKS, gathered):
-            o = attention(me, q, k_all, v_all, seq0, () if y is None else (y,))
-            y = project_o(o.reshape(n * tok, -1), w_o, x, y, seq0 * tok)
-            seq0 += n
+        for c, (k_all, v_all) in enumerate(gathered):
+            o = attention(me, q, k_all, v_all, c * n, () if y is None else (y,))
+            y = project_o(o.reshape(n * tok, -1), w_o, x, y, c * n * tok)
         return y.reshape(seqs, tok, d)
 
     rep_spec = P(None, None, None)

time: 932 us -> 893 us (0.958)
  Pallas kernels: 849 us -> 770 us
  waiting for transfers between devices: 2.51 us -> 33.3 us
    pallas_call x4, Pallas kernels: 330 us -> 263 us  [attention(): pl.pallas_call(attn_kernel, out_shape=jax.ShapeDtypeStruct((seqs, tok, q....]
    all_gather x4, waiting for transfers between devices: 0.01 us -> 29.6 us  [per_device(): lax.all_gather(v, 'cp', axis=0)]
    pallas_call x4 -> x2, Pallas kernels: 121 us -> 109 us  [project_kv(): pl.pallas_call(kv_kernel, out_shape=[jax.ShapeDtypeStruct((seqs, tok, n),...]
  transfers between devices with their start and end apart: 8 -> 8, of which waited for: 0 -> 1; matrix products, arithmetic and copies ran while one was open for 3% -> 3% of each run, Pallas kernels for 74% -> 71%
where the time goes in v3:
time: 893 us; the launch traced here: 879 us
  Pallas kernels  770 us (86%)
  local copies, waits for them, and re-layouts  50.1 us (6%)
  waiting for transfers between devices  33.3 us (4%)
  between operations  13.9 us (2%)
  other arithmetic  11.5 us (1%)
    pallas_call x4, Pallas kernels, attention(): pl.pallas_call(attn_kernel, out_shape=jax.ShapeDtypeStruct((seqs, tok, q....  263 us
    pallas_call x4, Pallas kernels, project_o(): pl.pallas_call(o_kernel, out_shape=jax.ShapeDtypeStruct((m, d), jnp.bfloa...  204 us
    pallas_call x1, Pallas kernels, project_q(): pl.pallas_call(q_kernel, out_shape=jax.ShapeDtypeStruct((m, n), jnp.bfloa...  194 us
    pallas_call x2, Pallas kernels, project_kv(): pl.pallas_call(kv_kernel, out_shape=[jax.ShapeDtypeStruct((seqs, tok, n),...  109 us
    unnamed x4, local copies, waits for them, and re-layouts  50.1 us
    all_gather x4, waiting for transfers between devices, per_device(): lax.all_gather(v, 'cp', axis=0)  29.6 us
  transfers between devices with their start and end apart: 8, of which 1 were waited for; matrix products, arithmetic and copies ran while one was open for 3% of the time, Pallas kernels for 71%

profile of v3, /device:TPU:6, one launch (start us, length us, event | category | flops | bytes accessed | tf_op | source)
XLA Modules:
  0.0 878.8 jit_solution(16806875994648454241)
XLA Ops:
  6.5 0.0 all-gather.31.cloned.1.call-start
  6.5 0.7 convert_bitcast_fusion
  7.3 10.8 %copy.19 = bf16[640,8,8,128]{3,1,2,0:T(8,128)(2,1)} copy(bf16[640,8,8,128]{3,2,1,0:T(8,128)(2,1)} %bitcast.45) | data formatting | bytes 20971520
  18.1 10.7 %copy.18 = bf16[640,8,8,128]{3,1,2,0:T(8,128)(2,1)} copy(bf16[640,8,8,128]{3,2,1,0:T(8,128)(2,1)} %bitcast.46) | data formatting | bytes 20971520
  28.8 7.7 fusion
  36.4 3.1 pad_maximum_fusion
  39.6 30.0 %project_kv.3 = (bf16[4,256,1024]{2,1,0:T(8,128)(2,1)}, bf16[4,1024,256]{2,1,0:T(8,128)(2,1)}) custom-call(bf16[4096,5120]{1,0:T(8,128)(2,1)} %bitcast.32, bf16[5120,1024]{1,0:T(8,128)(2,1)} %bitcast.47, bf16[5120,1024]{1,0:T(8,128)(2,1)} %bitcast.49, f32[4096,128]{1,0:T(8,128)} %get-tuple-element.26.cos_ref, f32[4096,128]{1,0:T(8,128)} %get-tuple-element.27.sin_ref), custom_call_target="tpu_custom_call" | custom-call | flops 21474836480 | bytes 35651584 | tf_op jit(solution)/shard_map/project_kv/pallas_call | solution.py:100
  69.6 0.0 all-gather.31.cloned.1.call-update
  69.7 0.0 all-gather.29.cloned.1.call-start
  69.7 0.7 all-gather.29.cloned.1.call-update
  70.4 0.0 all-gather.25.cloned.1.call-start
  70.4 79.2 %project_kv.2 = (bf16[4,256,1024]{2,1,0:T(8,128)(2,1)}, bf16[4,1024,256]{2,1,0:T(8,128)(2,1)}, bf16[4,256,1024]{2,1,0:T(8,128)(2,1)}, bf16[4,1024,256]{2,1,0:T(8...) custom-call(bf16[4096,5120]{1,0:T(8,128)(2,1)} %bitcast.33, bf16[5120,1024]{1,0:T(8,128)(2,1)} %bitcast.48, ...), custom_call_target="tpu_custom_call" | custom-call | flops 64424509440 | bytes 106954752 | tf_op jit(solution)/shard_map/project_kv/pallas_call | solution.py:100
  149.6 0.0 all-gather.25.cloned.1.call-update
  149.7 0.0 all-gather.27.cloned.1.call-start
  149.7 0.5 all-gather.27.cloned.1.call-update
  150.3 0.0 all-gather.21.cloned.1.call-start
  150.3 0.5 all-gather.21.cloned.1.call-update
  150.8 0.0 all-gather.23.cloned.1.call-start
  150.9 0.5 all-gather.23.cloned.1.call-update
  151.4 0.0 all-gather.17.cloned.1.call-start
  151.5 0.7 all-gather.17.cloned.1.call-update
  152.2 0.0 all-gather.19.cloned.1.call-start
  152.2 0.7 all-gather.19.cloned.1.call-update
  152.9 28.6 %copy.17 = bf16[640,8,32,128]{3,1,2,0:T(8,128)(2,1)} copy(bf16[640,8,32,128]{3,2,1,0:T(8,128)(2,1)} %bitcast.43) | data formatting | bytes 83886080
  181.6 193.8 %project_q.1 = bf16[4096,4096]{1,0:T(8,128)(2,1)} custom-call(bf16[4096,5120]{1,0:T(8,128)(2,1)} %bitcast.34, bf16[5120,4096]{1,0:T(8,128)(2,1)} %bitcast.44, f32[4096,128]{1,0:T(8,128)} %get-tuple-element.26.cos_ref, f32[4096,128]{1,0:T(8,128)} %get-tuple-element.27.sin_ref), custom_call_target="tpu_custom_call" | custom-call | flops 171798691840 | bytes 243269632 | tf_op jit(solution)/shard_map/project_q/pallas_call | solution.py:47
  375.4 0.0 all-gather.31.cloned.1.call-done
  375.4 0.0 all-gather.29.cloned.1.call-done
  375.4 65.5 %attention.4 = bf16[4,256,4096]{2,1,0:T(8,128)(2,1)} custom-call(s32[1]{0:T(128)} %bitcast.me_ref, bf16[16,256,4096]{2,1,0:T(8,128)(2,1)} %bitcast.63, bf16[8,4,256,1024]{3,2,1,0:T(8,128)(2,1)} %bitcast.56, bf16[8,4,1024,256]{3,2,1,0:T(8,128)(2,1)} %bitcast.55), custom_call_target="tpu_custom_call" | custom-call | flops 34359738368 | bytes 50331648 | tf_op jit(solution)/shard_map/attention/pallas_call | solution.py:179
  440.9 51.0 %project_o.4.rest_0_ = bf16[4096,5120]{1,0:T(8,128)(2,1)} custom-call(bf16[1024,4096]{1,0:T(8,128)(2,1)} %bitcast.67, bf16[4096,5120]{1,0:T(8,128)(2,1)} %bitcast.39, bf16[4096,5120]{1,0:T(8,128)(2,1)} %bitcast.35), custom_call_target="tpu_custom_call" | custom-call | flops 42949672960 | bytes 71303168 | tf_op jit(solution)/shard_map/project_o/pallas_call | solution.py:223
  491.9 0.0 all-gather.25.cloned.1.call-done
  491.9 0.0 all-gather.27.cloned.1.call-done
  491.9 65.8 %attention.5 = bf16[4,256,4096]{2,1,0:T(8,128)(2,1)} custom-call(s32[1]{0:T(128)} %bitcast.me_ref, bf16[16,256,4096]{2,1,0:T(8,128)(2,1)} %bitcast.64, bf16[8,4,256,1024]{3,2,1,0:T(8,128)(2,1)} %bitcast.57, bf16[8,4,1024,256]{3,2,1,0:T(8,128)(2,1)} %bitcast.59, bf16[4096,5120]{1,0:T(8,128)(2,1)} %project_o.4.rest_0_), custom_call_target="tpu_custom_call" | custom-call | flops 34359738368 | bytes 50331648 | tf_op jit(solution)/shard_map/attention/pallas_call | solution.py:179
  557.7 51.0 %project_o.5.rest_0_ = bf16[4096,5120]{1,0:T(8,128)(2,1)} custom-call(bf16[1024,4096]{1,0:T(8,128)(2,1)} %bitcast.52, bf16[4096,5120]{1,0:T(8,128)(2,1)} %bitcast.40, bf16[4096,5120]{1,0:T(8,128)(2,1)} %bitcast.36, bf16[4096,5120]{1,0:T(8,128)(2,1)} %project_o.4.rest_0_), custom_call_target="tpu_custom_call", output_to_operand_aliasing={{}: (3, {})} | custom-call | flops 42949672960 | bytes 71303168 | tf_op jit(solution)/shard_map/project_o/pallas_call | solution.py:223
  608.7 0.0 all-gather.21.cloned.1.call-done
  608.7 0.0 all-gather.23.cloned.1.call-done
  608.7 65.6 %attention.6 = bf16[4,256,4096]{2,1,0:T(8,128)(2,1)} custom-call(s32[1]{0:T(128)} %bitcast.me_ref, bf16[16,256,4096]{2,1,0:T(8,128)(2,1)} %bitcast.65, bf16[8,4,256,1024]{3,2,1,0:T(8,128)(2,1)} %bitcast.58, bf16[8,4,1024,256]{3,2,1,0:T(8,128)(2,1)} %bitcast.61, bf16[4096,5120]{1,0:T(8,128)(2,1)} %project_o.5.rest_0_), custom_call_target="tpu_custom_call" | custom-call | flops 34359738368 | bytes 50331648 | tf_op jit(solution)/shard_map/attention/pallas_call | solution.py:179
  674.3 51.0 %project_o.6.rest_0_ = bf16[4096,5120]{1,0:T(8,128)(2,1)} custom-call(bf16[1024,4096]{1,0:T(8,128)(2,1)} %bitcast.53, bf16[4096,5120]{1,0:T(8,128)(2,1)} %bitcast.41, bf16[4096,5120]{1,0:T(8,128)(2,1)} %bitcast.37, bf16[4096,5120]{1,0:T(8,128)(2,1)} %project_o.5.rest_0_), custom_call_target="tpu_custom_call", output_to_operand_aliasing={{}: (3, {})} | custom-call | flops 42949672960 | bytes 71303168 | tf_op jit(solution)/shard_map/project_o/pallas_call | solution.py:223
  725.3 0.0 all-gather.17.cloned.1.call-done
  725.3 29.6 %all-gather.19.cloned.1.call-done = bf16[32,1024,256]{2,1,0:T(8,128)(2,1)} async-done(((bf16[4,1024,256]{2,1,0:T(8,128)(2,1)}), bf16[32,1024,256]{2,1,0:T(8,128)(2,1)}) %all-gather.19.cloned.1.call-update) | async-done | bytes 16777232 | tf_op jit(solution)/shard_map/all_gather | solution.py:249
  754.9 65.6 %attention.7 = bf16[4,256,4096]{2,1,0:T(8,128)(2,1)} custom-call(s32[1]{0:T(128)} %bitcast.me_ref, bf16[16,256,4096]{2,1,0:T(8,128)(2,1)} %bitcast.66, bf16[8,4,256,1024]{3,2,1,0:T(8,128)(2,1)} %bitcast.60, bf16[8,4,1024,256]{3,2,1,0:T(8,128)(2,1)} %bitcast.62, bf16[4096,5120]{1,0:T(8,128)(2,1)} %project_o.6.rest_0_), custom_call_target="tpu_custom_call" | custom-call | flops 34359738368 | bytes 50331648 | tf_op jit(solution)/shard_map/attention/pallas_call | solution.py:179
  820.5 51.0 %project_o.7 = bf16[4096,5120]{1,0:T(8,128)(2,1)} custom-call(bf16[1024,4096]{1,0:T(8,128)(2,1)} %bitcast.51, bf16[4096,5120]{1,0:T(8,128)(2,1)} %bitcast.42, bf16[4096,5120]{1,0:T(8,128)(2,1)} %bitcast.38, bf16[4096,5120]{1,0:T(8,128)(2,1)} %project_o.6.rest_0_), custom_call_target="tpu_custom_call", output_to_operand_aliasing={{}: (3, {})} | custom-call | flops 42949672960 | bytes 71303168 | tf_op jit(solution)/shard_map/project_o/pallas_call | solution.py:223
  (2 shorter events, 0.0 us)
Async XLA Ops:
  6.5 368.9 %all-gather.31.cloned.1.call-start = ((), (), s32[]{:S(2)}) async-start(), calls=%async_computation.7 | async-start | bytes 18874368 | tf_op jit(solution)/shard_map/all_gather | solution.py:249
  69.7 305.7 %all-gather.29.cloned.1.call-start = ((), (), s32[]{:S(2)}) async-start(), calls=%async_computation.6 | async-start | bytes 18874368 | tf_op jit(solution)/shard_map/all_gather | solution.py:249
  70.4 421.5 %all-gather.25.cloned.1.call-start = ((), (), s32[]{:S(2)}) async-start(), calls=%async_computation.4 | async-start | bytes 18874368 | tf_op jit(solution)/shard_map/all_gather | solution.py:249
  149.7 342.2 %all-gather.27.cloned.1.call-start = ((), (), s32[]{:S(2)}) async-start(), calls=%async_computation.5 | async-start | bytes 18874368 | tf_op jit(solution)/shard_map/all_gather | solution.py:249
  150.3 458.5 %all-gather.21.cloned.1.call-start = ((), (), s32[]{:S(2)}) async-start(), calls=%async_computation.2 | async-start | bytes 18874368 | tf_op jit(solution)/shard_map/all_gather | solution.py:249
  150.8 457.9 %all-gather.23.cloned.1.call-start = ((), (), s32[]{:S(2)}) async-start(), calls=%async_computation.3 | async-start | bytes 18874368 | tf_op jit(solution)/shard_map/all_gather | solution.py:249
  151.4 573.9 %all-gather.17.cloned.1.call-start = ((), (), s32[]{:S(2)}) async-start(), calls=%async_computation | async-start | bytes 18874368 | tf_op jit(solution)/shard_map/all_gather | solution.py:249
  152.2 602.8 %all-gather.19.cloned.1.call-start = ((), (), s32[]{:S(2)}) async-start(), calls=%async_computation.1 | async-start | bytes 18874368 | tf_op jit(solution)/shard_map/all_gather | solution.py:249
Sparse Core Ops, SparseCore 0:
  69.8 84.0 all-gather.30
  155.7 84.0 all-gather.28
  241.6 84.0 all-gather.24
  327.4 84.0 all-gather.26
  413.2 84.0 all-gather.20
  499.0 84.0 all-gather.22
  584.9 84.0 all-gather.16
  670.8 84.0 all-gather.18
